TPU v7x, 32 devices: a whole 2x2x4 slice. The times are simulated.
32 devices in a mesh: gx: 2 (over y), gy: 8 (over z, core), gz: 2 (over x).
Axes of the slice: x: 2, y: 2, z: 4, core: 2. Of those that a mesh axis runs over, the one named last changes fastest.
Arguments:
- starting_kelvin: float32 [16, 32, 2048], P(None, 'gx', ('gy', 'gz')), may hold values from -6 to 6
- substance_label: int32 [16, 32, 2048], P(None, 'gx', ('gy', 'gz')), may hold values from 0 to 3
- voxel_source_patch: int32 [16, 32, 2048], P(None, 'gx', ('gy', 'gz')), may hold values from 0 to 15
- substance_traits: float32 [4, 4], replicated, may hold values from 0.5 to 2
- patch_source_intensity: float32 [16], replicated, may hold values from 0 to 8
Outputs:
- warmed_result: float32 [16, 32, 2048], P(None, 'gx', ('gy', 'gz'))
- solution: float32 [3, 16, 32, 2048], P(None, 'gz', 'gx', 'gy')
- residual: float32 [3, 16, 32, 2048], P(None, 'gz', 'gx', 'gy')
All inputs are finite; a program needn't handle non-finite values.
Results may differ from a plain program's by a relative error of at most 0.0029.
Values sent between devices are 32-bit elements; how exact they have to be, the bound alone decides.
A program may use at most 64 MiB of HBM per device.

v0:
```python
import jax
import jax.numpy as jnp
from jax import lax
from jax.sharding import PartitionSpec as P

ITERS = 3


time_step = 0.03
anchor_scale = 0.5
strain_gain = 2.0


def padded(value, sides, width):
    for axis, dim in sides:
        devices, length = (lax.axis_size(axis), value.shape[dim])
        up = [(i, (i + 1) % devices) for i in range(devices - 1)]
        down = [(j, i) for i, j in up]
        last = lax.slice_in_dim(value, length - width, length, axis=dim)
        initial = lax.slice_in_dim(value, 0, width, axis=dim)
        before = lax.ppermute(last, axis, up)
        after = lax.ppermute(initial, axis, down)
        value = jnp.concatenate([before, value, after], axis=dim)
    return value


def lookup(identity, table, count):
    summed = jnp.zeros(identity.shape, jnp.float32)
    for number in range(count):
        summed = summed + jnp.where(identity == number, table[number], jnp.float32(0.0))
    return summed


def conduct(own, other):
    return 2.0 * own * other / jnp.maximum(own + other, 0.25)


def heat_step(padded_temp, padded_cond, power, inverse_cap):
    centre = padded_temp[:, 1:-1, 1:-1]
    own = padded_cond[:, 1:-1, 1:-1]
    layers, rows, columns = centre.shape
    heat_flux = jnp.zeros_like(centre)
    for row_offset, column_offset in ((0, 1), (2, 1), (1, 0), (1, 2)):
        neighbour = padded_temp[
            :, row_offset : row_offset + rows, column_offset : column_offset + columns
        ]
        other = padded_cond[
            :, row_offset : row_offset + rows, column_offset : column_offset + columns
        ]
        heat_flux = heat_flux + conduct(own, other) * (neighbour - centre)
    vertical_temp = jnp.pad(centre, ((1, 1), (0, 0), (0, 0)))
    vertical_cond = jnp.pad(own, ((1, 1), (0, 0), (0, 0)))
    for layer_offset in (0, 2):
        other = vertical_cond[layer_offset : layer_offset + layers]
        neighbour = vertical_temp[layer_offset : layer_offset + layers]
        heat_flux = heat_flux + conduct(own, other) * (neighbour - centre)
    return centre + time_step * inverse_cap * (heat_flux + power)


def neighbour_offsets():
    listed = []
    for along_z in (-1, 0, 1):
        for along_x in (-1, 0, 1):
            for along_y in (-1, 0, 1):
                if along_z != 0 or along_x != 0 or along_y != 0:
                    listed.append((along_z, along_x, along_y))
    return listed


def apply_operator(field, padded_field, modulus, padded_modulus):
    layers, rows, columns = modulus.shape
    parts = [
        anchor_scale * modulus * field[0],
        anchor_scale * modulus * field[1],
        anchor_scale * modulus * field[2],
    ]
    for along_z, along_x, along_y in neighbour_offsets():
        length_sq = along_z * along_z + along_x * along_x + along_y * along_y
        window = (
            slice(1 + along_z, 1 + along_z + layers),
            slice(1 + along_x, 1 + along_x + rows),
            slice(1 + along_y, 1 + along_y + columns),
        )
        weight = 0.5 / length_sq * (modulus + padded_modulus[window])
        change = [field[index_c] - padded_field[index_c][window] for index_c in range(3)]
        projected = (along_z * change[0] + along_x * change[1] + along_y * change[2]) / length_sq
        for index_c, direction_part in enumerate((along_z, along_x, along_y)):
            parts[index_c] = parts[index_c] + weight * (
                0.5 * change[index_c] + direction_part * projected
            )
    return jnp.stack(parts)


def thermal_load(modulus, padded_modulus, strain, padded_strain):
    layers, rows, columns = modulus.shape
    parts = [jnp.zeros_like(modulus), jnp.zeros_like(modulus), jnp.zeros_like(modulus)]
    for along_z, along_x, along_y in neighbour_offsets():
        length_sq = along_z * along_z + along_x * along_x + along_y * along_y
        window = (
            slice(1 + along_z, 1 + along_z + layers),
            slice(1 + along_x, 1 + along_x + rows),
            slice(1 + along_y, 1 + along_y + columns),
        )
        weight = 0.5 / length_sq * (modulus + padded_modulus[window])
        pushing = weight * (0.5 * (strain + padded_strain[window]))
        for index_c, direction_part in enumerate((along_z, along_x, along_y)):
            if direction_part != 0:
                parts[index_c] = parts[index_c] - strain_gain * direction_part * pushing
    return jnp.stack(parts)


def two_products(residual, image):
    return lax.psum((jnp.sum(residual * residual), jnp.sum(residual * image)), ("gx", "gy", "gz"))


def per_device(
    starting_kelvin, substance_label, voxel_source_patch, substance_traits, patch_source_intensity
):
    count = substance_traits.shape[1]
    diffusive_coefficient = lookup(substance_label, substance_traits[0], count)
    inverse_cap = 1.0 / lookup(substance_label, substance_traits[1], count)
    power = lookup(voxel_source_patch, patch_source_intensity, patch_source_intensity.shape[0])
    padded_array = padded(
        jnp.stack([starting_kelvin, diffusive_coefficient]), (("gx", 2), (("gy", "gz"), 3)), 1
    )
    padded_cond = padded_array[1]
    warmed_result = heat_step(padded_array[0], padded_cond, power, inverse_cap)
    number = 0
    extended = padded(warmed_result, (("gx", 1), (("gy", "gz"), 2)), 1)
    warmed_result = heat_step(extended, padded_cond, power, inverse_cap)
    modulus = lookup(substance_label, substance_traits[2], count)
    strain = lookup(substance_label, substance_traits[3], count) * warmed_result
    fields = jnp.stack([modulus, strain])
    vertical_cycle = ((0, 0), (1, 1), (0, 0), (0, 0))
    padded_fields = jnp.pad(padded(fields, (("gx", 2), (("gy", "gz"), 3)), 1), vertical_cycle)

    def extend(field):
        return jnp.pad(padded(field, (("gx", 2), (("gy", "gz"), 3)), 1), vertical_cycle)

    modulus = fields[0]
    padded_modulus = padded_fields[0]
    load = thermal_load(modulus, padded_modulus, fields[1], padded_fields[1])

    def operate(field):
        return apply_operator(field, extend(field), modulus, padded_modulus)

    solution = jnp.zeros_like(load)
    residual = load
    image = operate(residual)
    norm_now, product = two_products(residual, image)
    alpha = norm_now / product
    direction, along_image = (residual, image)
    for number in range(ITERS):
        solution = solution + alpha * direction
        residual = residual - alpha * along_image
        if number + 1 < ITERS:
            image = operate(residual)
            norm_next, product = two_products(residual, image)
            ratio = norm_next / norm_now
            alpha = norm_next / (product - ratio * norm_next / alpha)
            direction = residual + ratio * direction
            along_image = image + ratio * along_image
            norm_now = norm_next
    joined = lax.all_to_all(
        jnp.concatenate([solution, residual]), "gz", split_axis=1, concat_axis=3, tiled=True
    )
    solution = joined[:3]
    residual = joined[3:]
    return (warmed_result, solution, residual)


def solution(mesh):
    in_specs = (
        P(None, "gx", ("gy", "gz")),
        P(None, "gx", ("gy", "gz")),
        P(None, "gx", ("gy", "gz")),
        P(),
        P(),
    )
    out_specs = (P(None, "gx", ("gy", "gz")), P(None, "gz", "gx", "gy"), P(None, "gz", "gx", "gy"))
    return jax.shard_map(
        per_device, mesh=mesh, in_specs=in_specs, out_specs=out_specs, check_vma=False
    )
```

profile of v0, /device:TPU:0, one launch (start us, length us, event | category | flops | bytes accessed | tf_op | source)
XLA Modules:
  0.0 370.7 jit_solution(7479689364601131842)
XLA Ops:
  9.6 4.9 %collective-permute-start = (f32[2,16,1,128]{3,1,2,0:T(8,128)S(1)}, f32[2,16,1,128]{3,1,2,0:T(8,128)S(1)}, u32[]{:S(2)}, u32[]{:S(2)}) collective-permute-start(f32[2,16,1,128]{3,1,2,0:T(8,128)S(1)} %get-tuple-element.112), channel_id=1, source_target_pairs={{0,16},{1,17},{2,18},{3,19},{4,20},{5,21},{6,22},{7,23},{8,24},{9,... | collective-permute-start | bytes 49160 | tf_op jit(solution)/shard_map/ppermute | solution.py:21
  15.9 4.2 %collective-permute-done.1 = f32[2,16,1,128]{3,1,2,0:T(8,128)S(1)} collective-permute-done((f32[2,16,1,128]{3,1,2,0:T(8,128)S(1)}, f32[2,16,1,128]{3,1,2,0:T(8,128)S(1)}, u32[]{:S(2)}, u32[]{:S(2)}) %collective-permute-start.1) | collective-permute-done | bytes 16416 | tf_op jit(solution)/shard_map/ppermute | solution.py:22
  25.8 8.3 %collective-permute-done.2 = f32[2,16,18,1]{3,1,2,0:T(8,128)S(1)} collective-permute-done((f32[2,16,18,1]{3,1,2,0:T(8,128)S(1)}, f32[2,16,18,1]{3,1,2,0:T(8,128)S(1)}, u32[]{:S(2)}, u32[]{:S(2)}) %collective-permute-start.2) | collective-permute-done | bytes 2336 | tf_op jit(solution)/shard_map/ppermute | solution.py:21
  35.3 13.0 %fusion.8 = f32[16,16,128]{2,0,1:T(8,128)S(1)} fusion(f32[16,16,128]{2,0,1:T(8,128)S(1)} %slice.2049, f32[16,18,130]{2,0,1:T(8,128)S(1)} %get-tuple-element.91, pred[16,16,128]{2,0,1:T(8,128)(4,1)S(1)} %get-tuple-element.74, f32[]{:T(128)} %bitcast.10, pred[16,16,128]{2,0,1:T(8,128)(4,1)S(1)} %get-tuple-element.73, f32[]{:T(128)} %bitcast.9, ...), kind=kLoop, calls=%fused_computation.73 | loop fusion | flops 3342336 | bytes 1835088 | tf_op jit(solution)/shard_map/add | solution.py:57
  51.3 4.2 %collective-permute-done.5 = f32[16,1,128]{2,0,1:T(8,128)S(1)} collective-permute-done((f32[16,1,128]{2,0,1:T(8,128)S(1)}, f32[16,1,128]{2,0,1:T(8,128)S(1)}, u32[]{:S(2)}, u32[]{:S(2)}) %collective-permute-start.5) | collective-permute-done | bytes 8224 | tf_op jit(solution)/shard_map/ppermute | solution.py:22
  55.6 4.8 %collective-permute-start.6 = (f32[16,18,1]{2,0,1:T(8,128)S(1)}, f32[16,18,1]{2,0,1:T(8,128)S(1)}, u32[]{:S(2)}, u32[]{:S(2)}) collective-permute-start(f32[16,18,1]{2,0,1:T(8,128)S(1)} %get-tuple-element.114), channel_id=1, source_target_pairs={{0,1},{1,2},{2,3},{3,4},{4,5},{5,6},{6,7},{7,8},{8,9},{9,10},{10,1... | collective-permute-start | bytes 3464 | tf_op jit(solution)/shard_map/ppermute | solution.py:21
  63.3 5.1 %collective-permute-done.7 = f32[16,18,1]{2,0,1:T(8,128)S(1)} collective-permute-done((f32[16,18,1]{2,0,1:T(8,128)S(1)}, f32[16,18,1]{2,0,1:T(8,128)S(1)}, u32[]{:S(2)}, u32[]{:S(2)}) %collective-permute-start.7) | collective-permute-done | bytes 1184 | tf_op jit(solution)/shard_map/ppermute | solution.py:22
  68.3 15.6 %add_multiply_fusion.6 = (f32[16,16,128]{2,0,1:T(8,128)S(1)}, f32[16,16,128]{2,0,1:T(8,128)S(1)}) fusion(pred[16,16,128]{2,0,1:T(8,128)(4,1)S(1)} %get-tuple-element.74, pred[16,16,128]{2,0,1:T(8,128)(4,1)S(1)} %get-tuple-element.73, pred[16,16,128]{2,0,1:T(8,128)(4,1)S(1)} %get-tuple-element.72, pred[16,16,128]{2,0,1:T(8,128)(4,1)S(1)} %get-tuple-element.71, ...), kind=kLoop, calls=%fused_computation.625 | loop fusion | flops 3866624 | bytes 1460576 | tf_op jit(solution)/shard_map/mul | solution.py:132
  87.0 4.2 %collective-permute-done.9 = f32[2,16,1,128]{3,1,2,0:T(8,128)S(1)} collective-permute-done((f32[2,16,1,128]{3,1,2,0:T(8,128)S(1)}, f32[2,16,1,128]{3,1,2,0:T(8,128)S(1)}, u32[]{:S(2)}, u32[]{:S(2)}) %collective-permute-start.9) | collective-permute-done | bytes 16416 | tf_op jit(solution)/shard_map/ppermute | solution.py:22
  94.1 5.2 %collective-permute-done.10 = f32[2,16,18,1]{3,1,2,0:T(8,128)S(1)} collective-permute-done((f32[2,16,18,1]{3,1,2,0:T(8,128)S(1)}, f32[2,16,18,1]{3,1,2,0:T(8,128)S(1)}, u32[]{:S(2)}, u32[]{:S(2)}) %collective-permute-start.10) | collective-permute-done | bytes 2336 | tf_op jit(solution)/shard_map/ppermute | solution.py:21
  99.3 4.7 %collective-permute-done.11 = f32[2,16,18,1]{3,1,2,0:T(8,128)S(1)} collective-permute-done((f32[2,16,18,1]{3,1,2,0:T(8,128)S(1)}, f32[2,16,18,1]{3,1,2,0:T(8,128)S(1)}, u32[]{:S(2)}, u32[]{:S(2)}) %collective-permute-start.11) | collective-permute-done | bytes 2336 | tf_op jit(solution)/shard_map/ppermute | solution.py:22
  118.4 4.2 %collective-permute-done.13 = f32[3,16,1,128]{3,1,2,0:T(8,128)S(1)} collective-permute-done((f32[3,16,1,128]{3,1,2,0:T(8,128)S(1)}, f32[3,16,1,128]{3,1,2,0:T(8,128)S(1)}, u32[]{:S(2)}, u32[]{:S(2)}) %collective-permute-start.13) | collective-permute-done | bytes 24608 | tf_op jit(solution)/shard_map/ppermute | solution.py:22
  123.3 6.3 %collective-permute-start.14 = (f32[3,16,18,1]{2,1,3,0:T(8,128)S(1)}, f32[3,16,18,1]{2,1,3,0:T(8,128)S(1)}, u32[]{:S(2)}, u32[]{:S(2)}) collective-permute-start(f32[3,16,18,1]{2,1,3,0:T(8,128)S(1)} %copy.174), channel_id=1, source_target_pairs={{0,1},{1,2},{2,3},{3,4},{4,5},{5,6},{6,7},{7,8},{8,9},{9,10},{10,1... | collective-permute-start | bytes 10376 | tf_op jit(solution)/shard_map/ppermute | solution.py:21
  131.9 3.9 %collective-permute-done.15 = f32[3,16,18,1]{2,1,3,0:T(8,128)S(1)} collective-permute-done((f32[3,16,18,1]{2,1,3,0:T(8,128)S(1)}, f32[3,16,18,1]{2,1,3,0:T(8,128)S(1)}, u32[]{:S(2)}, u32[]{:S(2)}) %collective-permute-start.15) | collective-permute-done | bytes 3488 | tf_op jit(solution)/shard_map/ppermute | solution.py:22
  137.0 5.2 %add_bitcast_fusion.7 = f32[1,16,16,128]{3,1,2,0:T(8,128)S(1)} fusion(f32[16,16,128]{2,0,1:T(8,128)S(1)} %fusion.52, f32[16,16,128]{2,0,1:T(8,128)S(1)} %fusion.93, f32[18,18,130]{2,0,1:T(8,128)S(1)} %get-tuple-element.85, f32[18,18,130]{2,0,1:T(8,128)S(1)} %get-tuple-element.84, f32[16,16,128]{2,0,1:T(8,128)S(1)} %fusion.31, ...), kind=kLoop, calls=%fused_computation.599 | loop fusion | flops 11862016 | bytes 14286864 | tf_op jit(solution)/shard_map/stack | solution.py:91
  142.2 5.2 %add_bitcast_fusion.6 = f32[1,16,16,128]{3,1,2,0:T(8,128)S(1)} fusion(f32[16,16,128]{2,0,1:T(8,128)S(1)} %fusion.31, f32[16,16,128]{2,0,1:T(8,128)S(1)} %fusion.93, f32[18,18,130]{2,0,1:T(8,128)S(1)} %get-tuple-element.85, f32[16,16,128]{2,0,1:T(8,128)S(1)} %fusion.52, f32[18,18,130]{2,0,1:T(8,128)S(1)} %get-tuple-element.84, ...), kind=kLoop, calls=%fused_computation.598 | loop fusion | flops 11862016 | bytes 14286864 | tf_op jit(solution)/shard_map/stack | solution.py:91
  147.4 5.2 %add_bitcast_fusion.8 = f32[1,16,16,128]{3,1,2,0:T(8,128)S(1)} fusion(f32[16,16,128]{2,0,1:T(8,128)S(1)} %fusion.93, f32[18,18,130]{2,0,1:T(8,128)S(1)} %get-tuple-element.85, f32[16,16,128]{2,0,1:T(8,128)S(1)} %fusion.52, f32[18,18,130]{2,0,1:T(8,128)S(1)} %get-tuple-element.84, f32[16,16,128]{2,0,1:T(8,128)S(1)} %fusion.31, ...), kind=kLoop, calls=%fused_computation.600 | loop fusion | flops 11862016 | bytes 14286864 | tf_op jit(solution)/shard_map/stack | solution.py:91
  153.3 40.6 %all-reduce.9 = (f32[]{:T(128)}, f32[]{:T(128)}) all-reduce(f32[]{:T(128)} %get-tuple-element.17, f32[]{:T(128)} %get-tuple-element.16), channel_id=1, replica_groups=mesh['gx'=2,'gy'=8,'gz'=2] {'gx','gy','gz'}, use_global_device_ids=true, to_apply=%region_1.2 | all-reduce | flops 2 | bytes 16 | tf_op jit(solution)/shard_map/psum | solution.py:113
  195.3 4.4 %collective-permute-start.16 = (f32[3,16,1,128]{3,1,2,0:T(8,128)S(1)}, f32[3,16,1,128]{3,1,2,0:T(8,128)S(1)}, u32[]{:S(2)}, u32[]{:S(2)}) collective-permute-start(f32[3,16,1,128]{3,1,2,0:T(8,128)S(1)} %get-tuple-element.102), channel_id=1, source_target_pairs={{0,16},{1,17},{2,18},{3,19},{4,20},{5,21},{6,22},{7,23},{8,24},{9,... | collective-permute-start | bytes 73736 | tf_op jit(solution)/shard_map/ppermute | solution.py:21
  201.2 4.2 %collective-permute-done.17 = f32[3,16,1,128]{3,1,2,0:T(8,128)S(1)} collective-permute-done((f32[3,16,1,128]{3,1,2,0:T(8,128)S(1)}, f32[3,16,1,128]{3,1,2,0:T(8,128)S(1)}, u32[]{:S(2)}, u32[]{:S(2)}) %collective-permute-start.17) | collective-permute-done | bytes 24608 | tf_op jit(solution)/shard_map/ppermute | solution.py:22
  210.4 3.8 %collective-permute-done.19 = f32[3,16,18,1]{2,1,3,0:T(8,128)S(1)} collective-permute-done((f32[3,16,18,1]{2,1,3,0:T(8,128)S(1)}, f32[3,16,18,1]{2,1,3,0:T(8,128)S(1)}, u32[]{:S(2)}, u32[]{:S(2)}) %collective-permute-start.19) | collective-permute-done | bytes 3488 | tf_op jit(solution)/shard_map/ppermute | solution.py:22
  215.3 5.4 %add_bitcast_fusion.5 = (f32[1,16,16,128]{3,1,2,0:T(8,128)S(1)}, f32[16,16,128]{2,0,1:T(8,128)S(1)}, f32[16,16,128]{2,0,1:T(8,128)S(1)}, f32[16,16,128]{2,0,1:T(...) fusion(f32[18,18,130]{2,0,1:T(8,128)S(1)} %get-tuple-element.82, ...), kind=kLoop, calls=%fused_computation.573 | loop fusion | flops 11862016 | bytes 17170448 | tf_op jit(solution)/shard_map/stack | solution.py:91
  220.7 4.1 %add_bitcast_fusion.4 = f32[1,16,16,128]{3,1,2,0:T(8,128)S(1)} fusion(f32[16,16,128]{2,0,1:T(8,128)S(1)} %get-tuple-element.69, f32[16,16,128]{2,0,1:T(8,128)S(1)} %get-tuple-element.51, f32[16,16,128]{2,0,1:T(8,128)S(1)} %get-tuple-element.66, f32[16,16,128]{2,0,1:T(8,128)S(1)} %get-tuple-element.50, f32[16,16,128]{2,0,1:T(8,128)S(1)} %get-tuple-element.65, ...), kind=kLoop, calls=%fused_computation.572 | loop fusion | flops 7864320 | bytes 11403280 | tf_op jit(solution)/shard_map/stack | solution.py:91
  224.8 4.1 %add_bitcast_fusion.3 = f32[1,16,16,128]{3,1,2,0:T(8,128)S(1)} fusion(f32[16,16,128]{2,0,1:T(8,128)S(1)} %get-tuple-element.69, f32[16,16,128]{2,0,1:T(8,128)S(1)} %get-tuple-element.68, f32[16,16,128]{2,0,1:T(8,128)S(1)} %get-tuple-element.67, f32[16,16,128]{2,0,1:T(8,128)S(1)} %get-tuple-element.66, f32[16,16,128]{2,0,1:T(8,128)S(1)} %get-tuple-element.65, ...), kind=kLoop, calls=%fused_computation.571 | loop fusion | flops 7864320 | bytes 11403280 | tf_op jit(solution)/shard_map/stack | solution.py:91
  229.7 39.7 %all-reduce.8 = (f32[]{:T(128)}, f32[]{:T(128)}) all-reduce(f32[]{:T(128)} %get-tuple-element.15, f32[]{:T(128)} %get-tuple-element.14), channel_id=1, replica_groups=mesh['gx'=2,'gy'=8,'gz'=2] {'gx','gy','gz'}, use_global_device_ids=true, to_apply=%region_5.6 | all-reduce | flops 2 | bytes 16 | tf_op jit(solution)/shard_map/psum | solution.py:113
  274.2 4.4 %collective-permute-start.20 = (f32[3,16,1,128]{3,1,2,0:T(8,128)S(1)}, f32[3,16,1,128]{3,1,2,0:T(8,128)S(1)}, u32[]{:S(2)}, u32[]{:S(2)}) collective-permute-start(f32[3,16,1,128]{3,1,2,0:T(8,128)S(1)} %get-tuple-element.100), channel_id=1, source_target_pairs={{0,16},{1,17},{2,18},{3,19},{4,20},{5,21},{6,22},{7,23},{8,24},{9,... | collective-permute-start | bytes 73736 | tf_op jit(solution)/shard_map/ppermute | solution.py:21
  280.1 4.2 %collective-permute-done.21 = f32[3,16,1,128]{3,1,2,0:T(8,128)S(1)} collective-permute-done((f32[3,16,1,128]{3,1,2,0:T(8,128)S(1)}, f32[3,16,1,128]{3,1,2,0:T(8,128)S(1)}, u32[]{:S(2)}, u32[]{:S(2)}) %collective-permute-start.21) | collective-permute-done | bytes 24608 | tf_op jit(solution)/shard_map/ppermute | solution.py:22
  294.1 5.4 %add_bitcast_fusion.2 = (f32[1,16,16,128]{3,1,2,0:T(8,128)S(1)}, f32[16,16,128]{2,0,1:T(8,128)S(1)}, f32[16,16,128]{2,0,1:T(8,128)S(1)}, f32[16,16,128]{2,0,1:T(...) fusion(f32[18,18,130]{2,0,1:T(8,128)S(1)} %get-tuple-element.79, ...), kind=kLoop, calls=%fused_computation.546 | loop fusion | flops 11862016 | bytes 17170448 | tf_op jit(solution)/shard_map/stack | solution.py:91
  299.5 4.1 %add_bitcast_fusion.1 = f32[1,16,16,128]{3,1,2,0:T(8,128)S(1)} fusion(f32[16,16,128]{2,0,1:T(8,128)S(1)} %get-tuple-element.46, f32[16,16,128]{2,0,1:T(8,128)S(1)} %get-tuple-element.28, f32[16,16,128]{2,0,1:T(8,128)S(1)} %get-tuple-element.43, f32[16,16,128]{2,0,1:T(8,128)S(1)} %get-tuple-element.27, f32[16,16,128]{2,0,1:T(8,128)S(1)} %get-tuple-element.42, ...), kind=kLoop, calls=%fused_computation.545 | loop fusion | flops 7864320 | bytes 11403280 | tf_op jit(solution)/shard_map/stack | solution.py:91
  303.6 4.1 %add_bitcast_fusion = f32[1,16,16,128]{3,1,2,0:T(8,128)S(1)} fusion(f32[16,16,128]{2,0,1:T(8,128)S(1)} %get-tuple-element.46, f32[16,16,128]{2,0,1:T(8,128)S(1)} %get-tuple-element.45, f32[16,16,128]{2,0,1:T(8,128)S(1)} %get-tuple-element.44, f32[16,16,128]{2,0,1:T(8,128)S(1)} %get-tuple-element.43, f32[16,16,128]{2,0,1:T(8,128)S(1)} %get-tuple-element.42, ...), kind=kLoop, calls=%fused_computation.544 | loop fusion | flops 7864320 | bytes 11403280 | tf_op jit(solution)/shard_map/stack | solution.py:91
  308.6 39.8 %all-reduce.7 = (f32[]{:T(128)}, f32[]{:T(128)}) all-reduce(f32[]{:T(128)} %get-tuple-element.13, f32[]{:T(128)} %get-tuple-element.12), channel_id=1, replica_groups=mesh['gx'=2,'gy'=8,'gz'=2] {'gx','gy','gz'}, use_global_device_ids=true, to_apply=%region_9.10 | all-reduce | flops 2 | bytes 16 | tf_op jit(solution)/shard_map/psum | solution.py:113
  358.2 9.7 %all-to-all-done = f32[6,16,16,128]{3,2,0,1:T(8,128)S(1)} async-done(((f32[6,16,16,128]{3,2,0,1:T(8,128)}), f32[6,16,16,128]{3,2,0,1:T(8,128)S(1)}, u32[]{:S(2)}, u32[]{:S(2)}) %all-to-all-start) | async-done | bytes 786464 | tf_op jit(solution)/shard_map/all_to_all | solution.py:164
  (100 shorter events, 77.2 us)
Async XLA Ops:
  6.1 19.0 %copy-start.1 = (f32[16]{0:T(128)S(1)}, f32[16]{0:T(128)}, u32[]{:S(2)}) copy-start(f32[16]{0:T(128)} %param.9) | copy-start | bytes 196
  9.6 6.3 %collective-permute-start = (f32[2,16,1,128]{3,1,2,0:T(8,128)S(1)}, f32[2,16,1,128]{3,1,2,0:T(8,128)S(1)}, u32[]{:S(2)}, u32[]{:S(2)}) collective-permute-start(f32[2,16,1,128]{3,1,2,0:T(8,128)S(1)} %get-tuple-element.112), channel_id=1, source_target_pairs={{0,16},{1,17},{2,18},{3,19},{4,20},{5,21},{6,22},{7,23},{8,24},{9,... | collective-permute-start | bytes 49160 | tf_op jit(solution)/shard_map/ppermute | solution.py:21
  14.5 5.6 %collective-permute-start.1 = (f32[2,16,1,128]{3,1,2,0:T(8,128)S(1)}, f32[2,16,1,128]{3,1,2,0:T(8,128)S(1)}, u32[]{:S(2)}, u32[]{:S(2)}) collective-permute-start(f32[2,16,1,128]{3,1,2,0:T(8,128)S(1)} %get-tuple-element.113), channel_id=1, source_target_pairs={{16,0},{17,1},{18,2},{19,3},{20,4},{21,5},{22,6},{23,7},{24,8},{25... | collective-permute-start | bytes 49160 | tf_op jit(solution)/shard_map/ppermute | solution.py:22
  20.3 13.8 %collective-permute-start.2 = (f32[2,16,18,1]{3,1,2,0:T(8,128)S(1)}, f32[2,16,18,1]{3,1,2,0:T(8,128)S(1)}, u32[]{:S(2)}, u32[]{:S(2)}) collective-permute-start(f32[2,16,18,1]{3,1,2,0:T(8,128)S(1)} %get-tuple-element.108), channel_id=1, source_target_pairs={{0,1},{1,2},{2,3},{3,4},{4,5},{5,6},{6,7},{7,8},{8,9},{9,10},{10,1... | collective-permute-start | bytes 6920 | tf_op jit(solution)/shard_map/ppermute | solution.py:21
  23.7 11.0 %collective-permute-start.3 = (f32[2,16,18,1]{3,1,2,0:T(8,128)S(1)}, f32[2,16,18,1]{3,1,2,0:T(8,128)S(1)}, u32[]{:S(2)}, u32[]{:S(2)}) collective-permute-start(f32[2,16,18,1]{3,1,2,0:T(8,128)S(1)} %get-tuple-element.109), channel_id=1, source_target_pairs={{1,0},{2,1},{3,2},{4,3},{5,4},{6,5},{7,6},{8,7},{9,8},{10,9},{11,1... | collective-permute-start | bytes 6920 | tf_op jit(solution)/shard_map/ppermute | solution.py:22
  25.8 9.5 %copy-start = (s32[16,16,128]{2,1,0:T(8,128)S(1)}, s32[16,16,128]{2,1,0:T(8,128)}, u32[]{:S(2)}) copy-start(s32[16,16,128]{2,1,0:T(8,128)} %param.7) | copy-start | bytes 393220
  48.3 3.0 collective-permute-start.4
  49.9 5.5 %collective-permute-start.5 = (f32[16,1,128]{2,0,1:T(8,128)S(1)}, f32[16,1,128]{2,0,1:T(8,128)S(1)}, u32[]{:S(2)}, u32[]{:S(2)}) collective-permute-start(f32[16,1,128]{2,0,1:T(8,128)S(1)} %get-tuple-element.117), channel_id=1, source_target_pairs={{16,0},{17,1},{18,2},{19,3},{20,4},{21,5},{22,6},{23,7},{24,8},{25... | collective-permute-start | bytes 24584 | tf_op jit(solution)/shard_map/ppermute | solution.py:22
  55.6 7.7 %collective-permute-start.6 = (f32[16,18,1]{2,0,1:T(8,128)S(1)}, f32[16,18,1]{2,0,1:T(8,128)S(1)}, u32[]{:S(2)}, u32[]{:S(2)}) collective-permute-start(f32[16,18,1]{2,0,1:T(8,128)S(1)} %get-tuple-element.114), channel_id=1, source_target_pairs={{0,1},{1,2},{2,3},{3,4},{4,5},{5,6},{6,7},{7,8},{8,9},{9,10},{10,1... | collective-permute-start | bytes 3464 | tf_op jit(solution)/shard_map/ppermute | solution.py:21
  60.4 7.9 %collective-permute-start.7 = (f32[16,18,1]{2,0,1:T(8,128)S(1)}, f32[16,18,1]{2,0,1:T(8,128)S(1)}, u32[]{:S(2)}, u32[]{:S(2)}) collective-permute-start(f32[16,18,1]{2,0,1:T(8,128)S(1)} %get-tuple-element.115), channel_id=1, source_target_pairs={{1,0},{2,1},{3,2},{4,3},{5,4},{6,5},{7,6},{8,7},{9,8},{10,9},{11,1... | collective-permute-start | bytes 3464 | tf_op jit(solution)/shard_map/ppermute | solution.py:22
  83.9 3.1 collective-permute-start.8
  85.5 5.6 %collective-permute-start.9 = (f32[2,16,1,128]{3,1,2,0:T(8,128)S(1)}, f32[2,16,1,128]{3,1,2,0:T(8,128)S(1)}, u32[]{:S(2)}, u32[]{:S(2)}) collective-permute-start(f32[2,16,1,128]{3,1,2,0:T(8,128)S(1)} %get-tuple-element.111), channel_id=1, source_target_pairs={{16,0},{17,1},{18,2},{19,3},{20,4},{21,5},{22,6},{23,7},{24,8},{25... | collective-permute-start | bytes 49160 | tf_op jit(solution)/shard_map/ppermute | solution.py:22
  91.4 7.9 %collective-permute-start.10 = (f32[2,16,18,1]{3,1,2,0:T(8,128)S(1)}, f32[2,16,18,1]{3,1,2,0:T(8,128)S(1)}, u32[]{:S(2)}, u32[]{:S(2)}) collective-permute-start(f32[2,16,18,1]{3,1,2,0:T(8,128)S(1)} %get-tuple-element.106), channel_id=1, source_target_pairs={{0,1},{1,2},{2,3},{3,4},{4,5},{5,6},{6,7},{7,8},{8,9},{9,10},{10,1... | collective-permute-start | bytes 6920 | tf_op jit(solution)/shard_map/ppermute | solution.py:21
  92.8 11.1 %collective-permute-start.11 = (f32[2,16,18,1]{3,1,2,0:T(8,128)S(1)}, f32[2,16,18,1]{3,1,2,0:T(8,128)S(1)}, u32[]{:S(2)}, u32[]{:S(2)}) collective-permute-start(f32[2,16,18,1]{3,1,2,0:T(8,128)S(1)} %get-tuple-element.107), channel_id=1, source_target_pairs={{1,0},{2,1},{3,2},{4,3},{5,4},{6,5},{7,6},{8,7},{9,8},{10,9},{11,1... | collective-permute-start | bytes 6920 | tf_op jit(solution)/shard_map/ppermute | solution.py:22
  114.7 3.7 %collective-permute-start.12 = (f32[3,16,1,128]{3,1,2,0:T(8,128)S(1)}, f32[3,16,1,128]{3,1,2,0:T(8,128)S(1)}, u32[]{:S(2)}, u32[]{:S(2)}) collective-permute-start(f32[3,16,1,128]{3,1,2,0:T(8,128)S(1)} %get-tuple-element.104), channel_id=1, source_target_pairs={{0,16},{1,17},{2,18},{3,19},{4,20},{5,21},{6,22},{7,23},{8,24},{9,... | collective-permute-start | bytes 73736 | tf_op jit(solution)/shard_map/ppermute | solution.py:21
  116.9 5.7 %collective-permute-start.13 = (f32[3,16,1,128]{3,1,2,0:T(8,128)S(1)}, f32[3,16,1,128]{3,1,2,0:T(8,128)S(1)}, u32[]{:S(2)}, u32[]{:S(2)}) collective-permute-start(f32[3,16,1,128]{3,1,2,0:T(8,128)S(1)} %get-tuple-element.105), channel_id=1, source_target_pairs={{16,0},{17,1},{18,2},{19,3},{20,4},{21,5},{22,6},{23,7},{24,8},{25... | collective-permute-start | bytes 73736 | tf_op jit(solution)/shard_map/ppermute | solution.py:22
  123.3 8.2 %collective-permute-start.14 = (f32[3,16,18,1]{2,1,3,0:T(8,128)S(1)}, f32[3,16,18,1]{2,1,3,0:T(8,128)S(1)}, u32[]{:S(2)}, u32[]{:S(2)}) collective-permute-start(f32[3,16,18,1]{2,1,3,0:T(8,128)S(1)} %copy.174), channel_id=1, source_target_pairs={{0,1},{1,2},{2,3},{3,4},{4,5},{5,6},{6,7},{7,8},{8,9},{9,10},{10,1... | collective-permute-start | bytes 10376 | tf_op jit(solution)/shard_map/ppermute | solution.py:21
  130.0 5.8 %collective-permute-start.15 = (f32[3,16,18,1]{2,1,3,0:T(8,128)S(1)}, f32[3,16,18,1]{2,1,3,0:T(8,128)S(1)}, u32[]{:S(2)}, u32[]{:S(2)}) collective-permute-start(f32[3,16,18,1]{2,1,3,0:T(8,128)S(1)} %copy.175), channel_id=1, source_target_pairs={{1,0},{2,1},{3,2},{4,3},{5,4},{6,5},{7,6},{8,7},{9,8},{10,9},{11,1... | collective-permute-start | bytes 10376 | tf_op jit(solution)/shard_map/ppermute | solution.py:22
  195.3 5.9 %collective-permute-start.16 = (f32[3,16,1,128]{3,1,2,0:T(8,128)S(1)}, f32[3,16,1,128]{3,1,2,0:T(8,128)S(1)}, u32[]{:S(2)}, u32[]{:S(2)}) collective-permute-start(f32[3,16,1,128]{3,1,2,0:T(8,128)S(1)} %get-tuple-element.102), channel_id=1, source_target_pairs={{0,16},{1,17},{2,18},{3,19},{4,20},{5,21},{6,22},{7,23},{8,24},{9,... | collective-permute-start | bytes 73736 | tf_op jit(solution)/shard_map/ppermute | solution.py:21
  199.7 5.7 %collective-permute-start.17 = (f32[3,16,1,128]{3,1,2,0:T(8,128)S(1)}, f32[3,16,1,128]{3,1,2,0:T(8,128)S(1)}, u32[]{:S(2)}, u32[]{:S(2)}) collective-permute-start(f32[3,16,1,128]{3,1,2,0:T(8,128)S(1)} %get-tuple-element.103), channel_id=1, source_target_pairs={{16,0},{17,1},{18,2},{19,3},{20,4},{21,5},{22,6},{23,7},{24,8},{25... | collective-permute-start | bytes 73736 | tf_op jit(solution)/shard_map/ppermute | solution.py:22
  206.0 3.9 %collective-permute-start.18 = (f32[3,16,18,1]{2,1,3,0:T(8,128)S(1)}, f32[3,16,18,1]{2,1,3,0:T(8,128)S(1)}, u32[]{:S(2)}, u32[]{:S(2)}) collective-permute-start(f32[3,16,18,1]{2,1,3,0:T(8,128)S(1)} %copy.190), channel_id=1, source_target_pairs={{0,1},{1,2},{2,3},{3,4},{4,5},{5,6},{6,7},{7,8},{8,9},{9,10},{10,1... | collective-permute-start | bytes 10376 | tf_op jit(solution)/shard_map/ppermute | solution.py:21
  208.5 5.7 %collective-permute-start.19 = (f32[3,16,18,1]{2,1,3,0:T(8,128)S(1)}, f32[3,16,18,1]{2,1,3,0:T(8,128)S(1)}, u32[]{:S(2)}, u32[]{:S(2)}) collective-permute-start(f32[3,16,18,1]{2,1,3,0:T(8,128)S(1)} %copy.191), channel_id=1, source_target_pairs={{1,0},{2,1},{3,2},{4,3},{5,4},{6,5},{7,6},{8,7},{9,8},{10,9},{11,1... | collective-permute-start | bytes 10376 | tf_op jit(solution)/shard_map/ppermute | solution.py:22
  274.2 5.9 %collective-permute-start.20 = (f32[3,16,1,128]{3,1,2,0:T(8,128)S(1)}, f32[3,16,1,128]{3,1,2,0:T(8,128)S(1)}, u32[]{:S(2)}, u32[]{:S(2)}) collective-permute-start(f32[3,16,1,128]{3,1,2,0:T(8,128)S(1)} %get-tuple-element.100), channel_id=1, source_target_pairs={{0,16},{1,17},{2,18},{3,19},{4,20},{5,21},{6,22},{7,23},{8,24},{9,... | collective-permute-start | bytes 73736 | tf_op jit(solution)/shard_map/ppermute | solution.py:21
  278.6 5.7 %collective-permute-start.21 = (f32[3,16,1,128]{3,1,2,0:T(8,128)S(1)}, f32[3,16,1,128]{3,1,2,0:T(8,128)S(1)}, u32[]{:S(2)}, u32[]{:S(2)}) collective-permute-start(f32[3,16,1,128]{3,1,2,0:T(8,128)S(1)} %get-tuple-element.101), channel_id=1, source_target_pairs={{16,0},{17,1},{18,2},{19,3},{20,4},{21,5},{22,6},{23,7},{24,8},{25... | collective-permute-start | bytes 73736 | tf_op jit(solution)/shard_map/ppermute | solution.py:22
  285.0 3.9 %collective-permute-start.22 = (f32[3,16,18,1]{2,1,3,0:T(8,128)S(1)}, f32[3,16,18,1]{2,1,3,0:T(8,128)S(1)}, u32[]{:S(2)}, u32[]{:S(2)}) collective-permute-start(f32[3,16,18,1]{2,1,3,0:T(8,128)S(1)} %copy.192), channel_id=1, source_target_pairs={{0,1},{1,2},{2,3},{3,4},{4,5},{5,6},{6,7},{7,8},{8,9},{9,10},{10,1... | collective-permute-start | bytes 10376 | tf_op jit(solution)/shard_map/ppermute | solution.py:21
  287.3 5.7 %collective-permute-start.23 = (f32[3,16,18,1]{2,1,3,0:T(8,128)S(1)}, f32[3,16,18,1]{2,1,3,0:T(8,128)S(1)}, u32[]{:S(2)}, u32[]{:S(2)}) collective-permute-start(f32[3,16,18,1]{2,1,3,0:T(8,128)S(1)} %copy.193), channel_id=1, source_target_pairs={{1,0},{2,1},{3,2},{4,3},{5,4},{6,5},{7,6},{8,7},{9,8},{10,9},{11,1... | collective-permute-start | bytes 10376 | tf_op jit(solution)/shard_map/ppermute | solution.py:22
  353.9 14.0 %all-to-all-start = ((f32[6,16,16,128]{3,2,0,1:T(8,128)}), f32[6,16,16,128]{3,2,0,1:T(8,128)S(1)}, u32[]{:S(2)}, u32[]{:S(2)}) async-start(f32[6,16,16,128]{3,2,0,1:T(8,128)} %copy.186), calls=%async_computation | async-start | bytes 1572864 | tf_op jit(solution)/shard_map/all_to_all | solution.py:164
where the time goes:
time: 373 us; the launch traced here: 371 us
  blocking collectives  120 us (32%)
  other arithmetic  94.1 us (25%)
  waiting for transfers between devices  72.8 us (20%)
  starting transfers between devices  58.9 us (16%)
  local copies, waits for them, and re-layouts  13.6 us (4%)
  between operations  11.3 us (3%)
    psum x3, blocking collectives, two_products(): lax.psum((jnp.sum(residual * residual), jnp.sum(residual * image)), ('gx'...  120 us
    ppermute x12, waiting for transfers between devices, padded(): after = lax.ppermute(initial, axis, down)  47.1 us
    another operation x9, other arithmetic, apply_operator(): return jnp.stack(parts)  42.9 us
    ppermute x12, starting transfers between devices, padded(): before = lax.ppermute(last, axis, up)  39.2 us
    ppermute x12, starting transfers between devices, padded(): after = lax.ppermute(initial, axis, down)  16.1 us
    ppermute x12, waiting for transfers between devices, padded(): before = lax.ppermute(last, axis, up)  16 us
    mul x1, other arithmetic, per_device(): strain = lookup(substance_label, substance_traits[3], count) * warmed_result  15.6 us
    add x1, other arithmetic, heat_step(): return centre + time_step * inverse_cap * (heat_flux + power)  13 us
  transfers between devices with their start and end apart: 25, of which 21 were waited for; matrix products, arithmetic and copies ran while one was open for 1% of the time, Pallas kernels for 0%

commit v1 on v0

v1 whole, which is shorter than its diff:
```python
import functools

import jax
import jax.numpy as jnp
from jax import lax
from jax.experimental import pallas as pl
from jax.experimental.pallas import tpu as pltpu
from jax.sharding import PartitionSpec as P

ITERS = 3
HALO = 8
TIME_STEP = 0.03
ANCHOR = 0.5
K_TOTAL = 4 * 0.25 + 4 * 0.125 + 2 * (0.75 + 4 * 0.25 + 4 * 5.0 / 36.0)
MESH = pl.DeviceIdType.MESH
DIRECTIONS = [(dx, dc) for dx in (-1, 0, 1) for dc in (-1, 0, 1) if (dx, dc) != (0, 0)]


def shift(f, axis, step):
    return pltpu.roll(f, (-step) % f.shape[axis], axis)


def sums(f, axis):
    after, before = shift(f, axis, 1), shift(f, axis, -1)
    return after + before, after - before


def matrix_parts(f):
    sy, dy = sums(f, 1)
    sx, dx = sums(f, 0)
    sxsy, dxsy = sums(sy, 0)
    sxdy, dxdy = sums(dy, 0)
    return sx, sy, sxsy, dx * 0.125 + dxsy * (1.0 / 18.0), dy * 0.125 + sxdy * (1.0 / 18.0), dxdy


def diag_z(f, sx, sy, sxsy):
    near = 0.25 * (sx + sy)
    return near + 0.125 * sxsy, 0.75 * f + near + (5.0 / 36.0) * sxsy


def diag_x(f, sx, sy, sxsy):
    near = 0.25 * sy
    return 0.75 * sx + near + 0.25 * sxsy, 0.25 * (f + sx) + 0.125 * sy + (5.0 / 36.0) * sxsy


def diag_y(f, sx, sy, sxsy):
    near = 0.25 * sx
    return 0.75 * sy + near + 0.25 * sxsy, 0.25 * (f + sy) + 0.125 * sx + (5.0 / 36.0) * sxsy


def vector_stencil(uz, ux, uy):
    sx, sy, sxsy, ex, ey, _ = matrix_parts(uz)
    z0, z1 = diag_z(uz, sx, sy, sxsy)
    dif_x, dif_y = ex, ey
    sx, sy, sxsy, ex, _, cross_x = matrix_parts(ux)
    x0, x1 = diag_x(ux, sx, sy, sxsy)
    dif_z = ex
    sx, sy, sxsy, _, ey, cross_y = matrix_parts(uy)
    y0, y1 = diag_y(uy, sx, sy, sxsy)
    dif_z = dif_z + ey
    x0, x1 = x0 + 0.125 * cross_y, x1 + (1.0 / 18.0) * cross_y
    y0, y1 = y0 + 0.125 * cross_x, y1 + (1.0 / 18.0) * cross_x
    return (z0, x0, y0), (z1, x1, y1), (dif_z, dif_x, dif_y)


def gradient_stencil(f):
    sy, dy = sums(f, 1)
    sx, dx = sums(f, 0)
    sxsy, dxsy = sums(sy, 0)
    sxdy, _ = sums(dy, 0)
    zero = jnp.zeros_like(f)
    return (
        (zero, 0.5 * dx + 0.25 * dxsy, 0.5 * dy + 0.25 * sxdy),
        (zero, 0.25 * dx + (1.0 / 6.0) * dxsy, 0.25 * dy + (1.0 / 6.0) * sxdy),
        (0.5 * f + 0.25 * (sx + sy) + (1.0 / 6.0) * sxsy, zero, zero),
    )


def stream(layers, count, zero, planes, emit, extra):
    def body(p, carry):
        held, below, extra = carry
        same, both, diff = planes(p)
        out = [h + b + d for h, b, d in zip(held, both, diff)]
        extra = emit(p - 1, out, extra)
        held = [w + s for w, s in zip(below, same)]
        below = [b - d for b, d in zip(both, diff)]
        return held, below, extra

    zeros = [zero] * count
    return lax.fori_loop(1, layers + 2, body, (zeros, list(zeros), extra))[2]


def kernel(
    sizes,
    kelvin, label, patch, traits, power_table,
    warmed, solution, residual,
    temp, temp2, lab, pat, cond, mod, strain, mask, gx_s, gy_s, gz_s, rate_s, pow_s, mats,
    v, vrecv, pack_f, pack_i, got_f, got_i, red_src, red_buf,
    local_sem, send_sem, recv_sem, vsend_sem, vrecv_sem, rsend_sem, rrecv_sem,
):
    nx, ny, nz = sizes
    nc, total = ny * nz, nx * ny * nz
    layers, rows, cols = kelvin.shape
    share = layers // nz
    full_rows = rows + 2 * HALO
    shape = (full_rows, 2 * cols)
    ix, iy, iz = lax.axis_index("gx"), lax.axis_index("gy"), lax.axis_index("gz")
    ic = iy * nz + iz
    me = ix * nc + ic

    def coords(flat):
        return (flat // nc, (flat % nc) // nz, flat % nz)

    barrier = pltpu.get_barrier_semaphore()

    def greet(k, _):
        pl.semaphore_signal(
            barrier, inc=1, device_id=coords(lax.rem(me + k, total)), device_id_type=MESH
        )
        return 0

    lax.fori_loop(1, total, greet, 0)

    own = (slice(None), pl.ds(HALO, rows), pl.ds(0, cols))
    local = [
        pltpu.make_async_copy(a, b.at[own], local_sem.at[i])
        for i, (a, b) in enumerate(((kelvin, temp), (label, lab), (patch, pat)))
    ]
    for copy in local:
        copy.start()

    lane = lax.broadcasted_iota(jnp.int32, (rows, cols), 1)
    sources = (kelvin, label, patch)
    for side in (0, 1):
        for index, ref in enumerate(sources):
            packed = jnp.zeros((rows, cols), ref.dtype)
            for z in range(layers):
                amount = (HALO * z + (HALO if side else 0)) % cols
                piece = ref[z]
                piece = pltpu.roll(piece, amount, 1) if amount else piece
                packed = jnp.where(lane // HALO == z, piece, packed)
            if index == 0:
                pack_f[side] = packed
            else:
                pack_i[side, index - 1] = packed

    pl.semaphore_wait(barrier, total - 1)

    def transfers(number):
        dx, dc = DIRECTIONS[number]
        there = (lax.rem(ix + dx + nx, nx) * nc) + lax.rem(ic + dc + nc, nc)
        target = jnp.logical_and(
            jnp.logical_and(ix + dx >= 0, ix + dx < nx), jnp.logical_and(ic + dc >= 0, ic + dc < nc)
        )
        origin = jnp.logical_and(
            jnp.logical_and(ix - dx >= 0, ix - dx < nx), jnp.logical_and(ic - dc >= 0, ic - dc < nc)
        )
        if dx == 0:
            from_rows, to_rows = pl.ds(0, rows), pl.ds(HALO, rows)
        elif dx == 1:
            from_rows, to_rows = pl.ds(rows - HALO, HALO), pl.ds(0, HALO)
        else:
            from_rows, to_rows = pl.ds(0, HALO), pl.ds(HALO + rows, HALO)
        if dc == 0:
            pairs = [
                (ref.at[:, from_rows, :], ext.at[:, to_rows, pl.ds(0, cols)])
                for ref, ext in zip(sources, (temp, lab, pat))
            ]
        else:
            side = (dc + 1) // 2
            pairs = [(pack_f.at[side, from_rows, :], got_f.at[side, to_rows, :])]
            pairs += [
                (pack_i.at[side, i, from_rows, :], got_i.at[side, i, to_rows, :]) for i in (0, 1)
            ]
        copies = [
            pltpu.make_async_remote_copy(
                src_ref=a, dst_ref=b, send_sem=send_sem.at[number, i],
                recv_sem=recv_sem.at[number, i], device_id=coords(there), device_id_type=MESH,
            )
            for i, (a, b) in enumerate(pairs)
        ]
        return target, origin, copies, to_rows, dc

    moves = [transfers(i) for i in range(len(DIRECTIONS))]
    for target, _, copies, _, _ in moves:
        @pl.when(target)
        def _(copies=copies):
            for copy in copies:
                copy.start()

    for _, origin, _, to_rows, dc in moves:
        @pl.when(jnp.logical_not(origin))
        def _(to_rows=to_rows, dc=dc):
            if dc == 0:
                block = (layers, to_rows.size, cols)
                temp[:, to_rows, 0:cols] = jnp.zeros(block, jnp.float32)
                lab[:, to_rows, 0:cols] = jnp.full(block, -1, jnp.int32)
                pat[:, to_rows, 0:cols] = jnp.zeros(block, jnp.int32)
            else:
                side = (dc + 1) // 2
                block = (to_rows.size, cols)
                got_f[side, to_rows, :] = jnp.zeros(block, jnp.float32)
                got_i[side, 0, to_rows, :] = jnp.full(block, -1, jnp.int32)
                got_i[side, 1, to_rows, :] = jnp.zeros(block, jnp.int32)

    empty = jnp.zeros(shape, jnp.float32)
    for end in (0, layers + 1):
        for ref in (mod, strain, mask):
            ref[end] = empty
        for k in range(ITERS):
            for c in range(3):
                v[k, c, end] = empty
    for c in range(6):
        mats[c, 0] = empty
    cond[layers] = empty

    shift_scalar = 3.0 * (traits[2, 0] + traits[2, 1] + traits[2, 2] + traits[2, 3])
    inverse_shift = 1.0 / jnp.full((1, 2 * cols), shift_scalar, jnp.float32)

    for copy in local:
        copy.wait()
    for _, origin, copies, _, _ in moves:
        @pl.when(origin)
        def _(copies=copies):
            for copy in copies:
                copy.wait_recv()

    halo_lane = lax.broadcasted_iota(jnp.int32, (full_rows, cols), 1)
    materials = traits.shape[1]
    tiles = power_table.shape[0]

    def prepare(z, _):
        def unpack(left, right, outside):
            left = pltpu.roll(left, lax.rem(2 * cols - HALO - HALO * z, cols), 1)
            right = pltpu.roll(right, lax.rem(cols - HALO * z, cols), 1)
            rest = jnp.where(halo_lane >= cols - HALO, left, outside)
            return jnp.where(halo_lane < HALO, right, rest)

        temp[z, :, cols:] = unpack(got_f[1], got_f[0], jnp.float32(0.0))
        label_halo = unpack(got_i[1, 0], got_i[0, 0], jnp.int32(-1))
        patch_halo = unpack(got_i[1, 1], got_i[0, 1], jnp.int32(0))
        for part, ids, patches in (
            (pl.ds(0, cols), lab[z, :, 0:cols], pat[z, :, 0:cols]),
            (pl.ds(cols, cols), label_halo, patch_halo),
        ):
            values = [jnp.zeros(ids.shape, jnp.float32) for _ in range(4)]
            for m in range(materials):
                hit = ids == m
                values = [jnp.where(hit, traits[q, m], values[q]) for q in range(4)]
            inside = ids >= 0
            cond[z, :, part] = values[0]
            rate_s[z, :, part] = jnp.where(inside, TIME_STEP / jnp.where(inside, values[1], 1.0), 0.0)
            mod[z + 1, :, part] = values[2] * inverse_shift[:, 0:cols]
            strain[z + 1, :, part] = values[3]
            mask[z + 1, :, part] = jnp.where(inside, 1.0, 0.0)
            power = jnp.zeros(ids.shape, jnp.float32)
            for t in range(tiles):
                power = jnp.where(patches == t, power_table[t], power)
            pow_s[z, :, part] = power
        return 0

    lax.fori_loop(0, layers, prepare, 0)

    def conduct(a, b):
        return 2.0 * a * b / jnp.maximum(a + b, 0.25)

    def heat(z, flow_below, source, first):
        centre = source[z]
        if first:
            own_cond = cond[z]
            along_x = conduct(own_cond, shift(own_cond, 0, 1))
            along_y = conduct(own_cond, shift(own_cond, 1, 1))
            along_z = conduct(own_cond, cond[z + 1])
            gx_s[z], gy_s[z], gz_s[z] = along_x, along_y, along_z
        else:
            along_x, along_y, along_z = gx_s[z], gy_s[z], gz_s[z]
        flow_x = along_x * (shift(centre, 0, 1) - centre)
        flow_y = along_y * (shift(centre, 1, 1) - centre)
        flow_z = along_z * (source[jnp.minimum(z + 1, layers - 1)] - centre)
        flux = flow_x - shift(flow_x, 0, -1) + flow_y - shift(flow_y, 1, -1) + flow_z - flow_below
        return centre + rate_s[z] * (flux + pow_s[z]), flow_z

    def first_step(z, flow_below):
        temp2[z], flow_z = heat(z, flow_below, temp, True)
        return flow_z

    blank = mod[0]
    lax.fori_loop(0, layers, first_step, blank)

    def second_step(z, flow_below):
        value, flow_z = heat(z, flow_below, temp2, False)
        warmed[z] = value[HALO : HALO + rows, 0:cols]
        strain[z + 1] = strain[z + 1] * value
        return flow_z

    lax.fori_loop(0, layers, second_step, blank)

    def matrix_planes(p):
        f = mod[p]
        sx, sy, sxsy, ex, ey, cross = matrix_parts(f)
        z0, z1 = diag_z(f, sx, sy, sxsy)
        x0, x1 = diag_x(f, sx, sy, sxsy)
        y0, y1 = diag_y(f, sx, sy, sxsy)
        zero = jnp.zeros_like(f)
        return (
            (z0, x0, y0, zero, zero, 0.125 * cross),
            (z1, x1, y1, zero, zero, (1.0 / 18.0) * cross),
            (zero, zero, zero, ex, ey, zero),
        )

    def matrix_emit(p, out, extra):
        diagonal = (ANCHOR + K_TOTAL) * mod[p] - 1.0
        for c in range(6):
            mats[c, p] = out[c] + diagonal if c < 3 else out[c]
        return extra

    stream(layers, 6, blank, matrix_planes, matrix_emit, 0)

    def fold(value):
        inner = value[HALO : HALO + rows, 0:cols]
        result = inner[0:8]
        for r in range(8, rows, 8):
            result = result + inner[r : r + 8]
        return result

    tile = mod[0, 0:8, 0:cols]

    def load_planes(p):
        m, s = mod[p], strain[p]
        parts = [gradient_stencil(f) for f in (s, m, m * s)]
        return tuple(tuple(a for part in parts for a in part[i]) for i in range(3))

    def load_emit(p, out, acc):
        m, s, inside = mod[p], strain[p], mask[p]
        for c in range(3):
            value = -inside * (m * out[c] + s * out[3 + c] + out[6 + c])
            v[0, c, p] = value
            acc = acc + fold(value * value)
        return acc

    moments = [stream(layers, 9, blank, load_planes, load_emit, tile)]

    def shares(k):
        found = []
        for step in range(1, nz):
            there = lax.rem(iz + step, nz)
            found.append(
                pltpu.make_async_remote_copy(
                    src_ref=v.at[k, :, pl.ds(1 + there * share, share), pl.ds(HALO, rows), pl.ds(0, cols)],
                    dst_ref=vrecv.at[k, step - 1],
                    send_sem=vsend_sem.at[k, step - 1], recv_sem=vrecv_sem.at[k, step - 1],
                    device_id=(ix, iy, there), device_id_type=MESH,
                )
            )
        return found

    sharing = [shares(k) for k in range(ITERS + 1)]
    for copy in sharing[0]:
        copy.start()

    for k in range(ITERS):
        def planes(p, k=k):
            m = mod[p]
            u = [v[k, c, p] for c in range(3)]
            first = vector_stencil(*u)
            second = vector_stencil(*[m * f for f in u])
            return tuple(a + b for a, b in zip(first, second))

        def emit(p, out, acc, k=k):
            m, inside = mod[p], mask[p]
            u = [v[k, c, p] for c in range(3)]
            zz, xx, yy, zx, zy, xy = [mats[c, p] for c in range(6)]
            grown = (
                zz * u[0] + zx * u[1] + zy * u[2],
                zx * u[0] + xx * u[1] + xy * u[2],
                zy * u[0] + xy * u[1] + yy * u[2],
            )
            odd, even = acc
            for c in range(3):
                value = inside * (grown[c] - m * out[c] - out[3 + c])
                v[k + 1, c, p] = value
                odd = odd + fold(value * u[c])
                even = even + fold(value * value)
            return odd, even

        odd, even = stream(layers, 6, blank, planes, emit, (tile, tile))
        moments += [odd, even]
        for copy in sharing[k + 1]:
            copy.start()

    moments = moments[: 2 * ITERS]
    lane8 = lax.broadcasted_iota(jnp.int32, (1, cols), 1)
    row = jnp.zeros((1, cols), jnp.float32)
    for k, value in enumerate(moments):
        line = jnp.sum(value, axis=0, keepdims=True)
        row = jnp.where(lane8 == k, jnp.sum(line, axis=1, keepdims=True), row)
    red_src[...] = row
    red_buf[me] = row

    def spread(k):
        there = lax.rem(me + k, total)
        return pltpu.make_async_remote_copy(
            src_ref=red_src, dst_ref=red_buf.at[me], send_sem=rsend_sem.at[k],
            recv_sem=rrecv_sem.at[k], device_id=coords(there), device_id_type=MESH,
        )

    def collect(k):
        there = lax.rem(me + total - k, total)
        return pltpu.make_async_remote_copy(
            src_ref=red_src, dst_ref=red_buf.at[there], send_sem=rsend_sem.at[k],
            recv_sem=rrecv_sem.at[k], device_id=coords(there), device_id_type=MESH,
        )

    def start(k, _):
        spread(k).start()
        return 0

    def finish(k, _):
        collect(k).wait_recv()
        return 0

    def sent(k, _):
        spread(k).wait_send()
        return 0

    lax.fori_loop(1, total, start, 0)
    lax.fori_loop(1, total, finish, 0)

    def add(k, acc):
        return acc + red_buf[k]

    summed = lax.fori_loop(0, total, add, jnp.zeros((1, cols), jnp.float32))
    m = [
        jnp.sum(jnp.where(lane8 == k, summed, 0.0), axis=1, keepdims=True) for k in range(2 * ITERS)
    ]

    def inner(a, b):
        value = None
        for i, x in enumerate(a):
            for j, y in enumerate(b):
                if x is not None and y is not None:
                    term = x * y * m[i + j]
                    value = term if value is None else value + term
        return value

    def plus(a, factor, b):
        out = []
        for x, y in zip(a, b):
            if y is None:
                out.append(x)
            else:
                out.append(factor * y if x is None else x + factor * y)
        return out

    one = jnp.ones((1, 1), jnp.float32)
    size = ITERS + 1
    res = [one] + [None] * ITERS
    dire = list(res)
    sol = [None] * size
    rr = m[0]
    for number in range(ITERS):
        image = plus(list(dire), 1.0, [None] + dire[:-1])
        alpha = rr / inner(dire, image)
        sol = plus(sol, alpha, dire)
        res = plus(res, -alpha, image)
        if number + 1 < ITERS:
            new = inner(res, res)
            dire = plus(res, new / rr, dire)
            rr = new
    res = [shift_scalar * x for x in res]

    for k in range(ITERS + 1):
        for copy in sharing[k]:
            copy.wait_recv()

    for step in range(nz):
        where = pl.ds(pl.multiple_of(lax.rem(iz + nz - step, nz) * cols, cols), cols)

        def combine(z, _, step=step, where=where):
            for c in range(3):
                if step == 0:
                    parts = [
                        v[k, c, 1 + iz * share + z, pl.ds(HALO, rows), pl.ds(0, cols)]
                        for k in range(size)
                    ]
                else:
                    parts = [vrecv[k, step - 1, c, z] for k in range(size)]
                total_s = sol[0] * parts[0]
                total_r = res[0] * parts[0]
                for k in range(1, size):
                    if sol[k] is not None:
                        total_s = total_s + sol[k] * parts[k]
                    total_r = total_r + res[k] * parts[k]
                solution[c, z, :, where] = total_s
                residual[c, z, :, where] = total_r
            return 0

        lax.fori_loop(0, share, combine, 0)

    for target, _, copies, _, _ in moves:
        @pl.when(target)
        def _(copies=copies):
            for copy in copies:
                copy.wait_send()
    for k in range(ITERS + 1):
        for copy in sharing[k]:
            copy.wait_send()
    lax.fori_loop(1, total, sent, 0)


def per_device(sizes, *arrays):
    nx, ny, nz = sizes
    layers, rows, cols = arrays[0].shape
    total = nx * ny * nz
    share = layers // nz
    ext = (rows + 2 * HALO, 2 * cols)
    f32, i32 = jnp.float32, jnp.int32
    vmem = pltpu.VMEM
    dma = pltpu.SemaphoreType.DMA
    out = jax.ShapeDtypeStruct((3, share, rows, cols * nz), f32)
    plane = vmem((layers, *ext), f32)
    padded = vmem((layers + 2, *ext), f32)
    return pl.pallas_call(
        functools.partial(kernel, sizes),
        out_shape=(jax.ShapeDtypeStruct((layers, rows, cols), f32), out, out),
        in_specs=[pl.BlockSpec(memory_space=pltpu.VMEM)] * 3
        + [pl.BlockSpec(memory_space=pltpu.SMEM)] * 2,
        out_specs=[pl.BlockSpec(memory_space=pltpu.VMEM)] * 3,
        scratch_shapes=[
            plane, plane, vmem((layers, *ext), i32), vmem((layers, *ext), i32),
            vmem((layers + 1, *ext), f32), padded, padded, padded,
            plane, plane, plane, plane, plane,
            vmem((6, layers + 1, *ext), f32),
            vmem((ITERS + 1, 3, layers + 2, *ext), f32),
            vmem((ITERS + 1, nz - 1, 3, share, rows, cols), f32),
            vmem((2, rows, cols), f32), vmem((2, 2, rows, cols), i32),
            vmem((2, ext[0], cols), f32), vmem((2, 2, ext[0], cols), i32),
            vmem((1, cols), f32), vmem((total, 1, cols), f32),
            dma((3,)), dma((8, 3)), dma((8, 3)),
            dma((ITERS + 1, nz - 1)), dma((ITERS + 1, nz - 1)), dma((total,)), dma((total,)),
        ],
        compiler_params=pltpu.CompilerParams(
            collective_id=0, has_side_effects=True, vmem_limit_bytes=60 * 1024 * 1024
        ),
    )(*arrays)


def solution(mesh):
    sizes = tuple(mesh.shape[axis] for axis in ("gx", "gy", "gz"))
    split = P(None, "gx", ("gy", "gz"))
    out = P(None, "gz", "gx", "gy")
    return jax.shard_map(
        functools.partial(per_device, sizes),
        mesh=mesh,
        in_specs=(split, split, split, P(), P()),
        out_specs=(split, out, out),
        check_vma=False,
    )
```

time: 373 us -> 65.7 us (0.18)
  blocking collectives: 120 us -> 0 us
  other arithmetic: 94.1 us -> 0 us
  waiting for transfers between devices: 72.8 us -> 0 us
  Pallas kernels: 0 us -> 60.7 us
  starting transfers between devices: 58.9 us -> 0 us
  between operations: 11.3 us -> 0.64 us
  local copies, waits for them, and re-layouts: 13.6 us -> 4.13 us
    psum x3 -> x0, blocking collectives: 120 us -> none  [two_products(): lax.psum((jnp.sum(residual * residual), jnp.sum(residual * image)), ('gx'...]
    ppermute x24 -> x0, waiting for transfers between devices: 63 us -> none  [the longest x12 47.1 us: padded(): after = lax.ppermute(initial, axis, down)]
    pallas_call x0 -> x1, Pallas kernels: none -> 60.7 us  [per_device(): pl.pallas_call(functools.partial(kernel, sizes), out_shape=(jax.ShapeDtyp...]
    ppermute x24 -> x0, starting transfers between devices: 55.3 us -> none  [the longest x12 39.2 us: padded(): before = lax.ppermute(last, axis, up)]
    another operation x12 -> x0, other arithmetic: 49.9 us -> none  [the longest x9 42.9 us: apply_operator(): return jnp.stack(parts)]
    mul x1 -> x0, other arithmetic: 15.6 us -> none  [per_device(): strain = lookup(substance_label, substance_traits[3], count) * warmed_result]
    add x2 -> x0, other arithmetic: 13.2 us -> none  [the longest x1 13 us: heat_step(): return centre + time_step * inverse_cap * (heat_flux + power)]
    sub x5 -> x0, other arithmetic: 10.3 us -> none  [the longest x3 10.2 us: thermal_load(): parts[index_c] = parts[index_c] - strain_gain * direction_part * pushing]
  transfers between devices with their start and end apart: 25 -> 0, of which waited for: 21 -> 0; matrix products, arithmetic and copies ran while one was open for 1% -> 0% of each run, Pallas kernels for 0% -> 0%
where the time goes in v1:
time: 65.7 us; the launch traced here: 65.5 us
  Pallas kernels  60.7 us (92%)
  local copies, waits for them, and re-layouts  4.13 us (6%)
    pallas_call x1, Pallas kernels, per_device(): pl.pallas_call(functools.partial(kernel, sizes), out_shape=(jax.ShapeDtyp...  60.7 us
    unnamed x5, local copies, waits for them, and re-layouts  4.13 us

profile of v1, /device:TPU:0, one launch (start us, length us, event | category | flops | bytes accessed | tf_op | source)
XLA Modules:
  0.0 65.5 jit_solution(6188270482381335104)
XLA Ops:
  0.6 60.7 %shard_map.76 = (f32[16,16,128]{2,1,0:T(8,128)}, f32[3,8,16,256]{3,2,1,0:T(8,128)}, f32[3,8,16,256]{3,2,1,0:T(8,128)}) custom-call(f32[16,16,128]{2,1,0:T(8,128)} %kelvin.1, s32[16,16,128]{2,1,0:T(8,128)} %label.1, s32[16,16,128]{2,1,0:T(8,128)} %patch.1, f32[4,4]{1,0:T(4,128)} %traits.1, f32[16]{0:T(128)} %power_table.1), custom_call_target="tpu_custom_call" | custom-call | tf_op jit(solution)/shard_map/pallas_call | solution.py:523
  61.3 1.6 %copy.11 = f32[16,16,128]{2,1,0:T(8,128)} copy(f32[16,16,128]{2,1,0:T(8,128)} %get-tuple-element.6) | data formatting | bytes 262144
  62.9 0.0 copy-start
  62.9 1.8 %copy.12 = f32[3,8,16,256]{3,2,1,0:T(8,128)} copy(f32[3,8,16,256]{3,2,1,0:T(8,128)} %get-tuple-element.7) | data formatting | bytes 786432
  64.7 0.0 copy-done
  64.7 0.7 %copy.13 = f32[3,8,16,256]{3,2,1,0:T(8,128)} copy(f32[3,8,16,256]{3,2,1,0:T(8,128)S(1)} %copy-done) | data formatting | bytes 786432
Async XLA Ops:
  62.9 1.8 %copy-start = (f32[3,8,16,256]{3,2,1,0:T(8,128)S(1)}, f32[3,8,16,256]{3,2,1,0:T(8,128)}, u32[]{:S(2)}) copy-start(f32[3,8,16,256]{3,2,1,0:T(8,128)} %get-tuple-element.8) | copy-start | bytes 1179652

commit v2 on v1

--- a/solution.py
+++ b/solution.py
@@ -9,6 +9,7 @@
 
 ITERS = 3
 HALO = 8
+EDGE = 4
 TIME_STEP = 0.03
 ANCHOR = 0.5
 K_TOTAL = 4 * 0.25 + 4 * 0.125 + 2 * (0.75 + 4 * 0.25 + 4 * 5.0 / 36.0)
@@ -25,8 +26,10 @@
     return after + before, after - before
 
 
-def matrix_parts(f):
+def matrix_parts(f, width=None):
     sy, dy = sums(f, 1)
+    if width is not None:
+        f, sy, dy = f[:, :width], sy[:, :width], dy[:, :width]
     sx, dx = sums(f, 0)
     sxsy, dxsy = sums(sy, 0)
     sxdy, dxdy = sums(dy, 0)
@@ -48,15 +51,16 @@
     return 0.75 * sy + near + 0.25 * sxsy, 0.25 * (f + sy) + 0.125 * sx + (5.0 / 36.0) * sxsy
 
 
-def vector_stencil(uz, ux, uy):
-    sx, sy, sxsy, ex, ey, _ = matrix_parts(uz)
+def vector_stencil(uz, ux, uy, width):
+    sx, sy, sxsy, ex, ey, _ = matrix_parts(uz, width)
+    uz, ux_in, uy_in = uz[:, :width], ux[:, :width], uy[:, :width]
     z0, z1 = diag_z(uz, sx, sy, sxsy)
     dif_x, dif_y = ex, ey
-    sx, sy, sxsy, ex, _, cross_x = matrix_parts(ux)
-    x0, x1 = diag_x(ux, sx, sy, sxsy)
+    sx, sy, sxsy, ex, _, cross_x = matrix_parts(ux, width)
+    x0, x1 = diag_x(ux_in, sx, sy, sxsy)
     dif_z = ex
-    sx, sy, sxsy, _, ey, cross_y = matrix_parts(uy)
-    y0, y1 = diag_y(uy, sx, sy, sxsy)
+    sx, sy, sxsy, _, ey, cross_y = matrix_parts(uy, width)
+    y0, y1 = diag_y(uy_in, sx, sy, sxsy)
     dif_z = dif_z + ey
     x0, x1 = x0 + 0.125 * cross_y, x1 + (1.0 / 18.0) * cross_y
     y0, y1 = y0 + 0.125 * cross_x, y1 + (1.0 / 18.0) * cross_x
@@ -93,7 +97,8 @@
 def kernel(
     sizes,
     kelvin, label, patch, traits, power_table,
-    warmed, solution, residual,
+    warmed_out, solution_out, residual_out,
+    warmed, solution, residual, vown, moment_s, out_sem,
     temp, temp2, lab, pat, cond, mod, strain, mask, gx_s, gy_s, gz_s, rate_s, pow_s, mats,
     v, vrecv, pack_f, pack_i, got_f, got_i, red_src, red_buf,
     local_sem, send_sem, recv_sem, vsend_sem, vrecv_sem, rsend_sem, rrecv_sem,
@@ -104,6 +109,8 @@
     share = layers // nz
     full_rows = rows + 2 * HALO
     shape = (full_rows, 2 * cols)
+    kept = slice(HALO - EDGE, HALO + rows + EDGE)
+    inner_rows = slice(EDGE, EDGE + rows)
     ix, iy, iz = lax.axis_index("gx"), lax.axis_index("gy"), lax.axis_index("gz")
     ic = iy * nz + iz
     me = ix * nc + ic
@@ -131,12 +138,14 @@
 
     lane = lax.broadcasted_iota(jnp.int32, (rows, cols), 1)
     sources = (kelvin, label, patch)
+    for copy in local:
+        copy.wait()
     for side in (0, 1):
-        for index, ref in enumerate(sources):
+        for index, ref in enumerate((temp, lab, pat)):
             packed = jnp.zeros((rows, cols), ref.dtype)
             for z in range(layers):
                 amount = (HALO * z + (HALO if side else 0)) % cols
-                piece = ref[z]
+                piece = ref[(z, *own[1:])]
                 piece = pltpu.roll(piece, amount, 1) if amount else piece
                 packed = jnp.where(lane // HALO == z, piece, packed)
             if index == 0:
@@ -204,21 +213,20 @@
                 got_i[side, 1, to_rows, :] = jnp.zeros(block, jnp.int32)
 
     empty = jnp.zeros(shape, jnp.float32)
+    blank_kept = jnp.zeros((rows + 2 * EDGE, 2 * cols), jnp.float32)
     for end in (0, layers + 1):
         for ref in (mod, strain, mask):
-            ref[end] = empty
+            ref[end] = blank_kept
         for k in range(ITERS):
             for c in range(3):
-                v[k, c, end] = empty
+                v[k, c, end] = blank_kept
     for c in range(6):
-        mats[c, 0] = empty
+        mats[c, 0] = blank_kept
     cond[layers] = empty
 
     shift_scalar = 3.0 * (traits[2, 0] + traits[2, 1] + traits[2, 2] + traits[2, 3])
     inverse_shift = 1.0 / jnp.full((1, 2 * cols), shift_scalar, jnp.float32)
 
-    for copy in local:
-        copy.wait()
     for _, origin, copies, _, _ in moves:
         @pl.when(origin)
         def _(copies=copies):
@@ -243,16 +251,18 @@
             (pl.ds(0, cols), lab[z, :, 0:cols], pat[z, :, 0:cols]),
             (pl.ds(cols, cols), label_halo, patch_halo),
         ):
-            values = [jnp.zeros(ids.shape, jnp.float32) for _ in range(4)]
+            near = ids[kept]
+            values = [jnp.zeros(a.shape, jnp.float32) for a in (ids, ids, near, near)]
             for m in range(materials):
-                hit = ids == m
-                values = [jnp.where(hit, traits[q, m], values[q]) for q in range(4)]
+                hit, near_hit = ids == m, near == m
+                hits = (hit, hit, near_hit, near_hit)
+                values = [jnp.where(hits[q], traits[q, m], values[q]) for q in range(4)]
             inside = ids >= 0
             cond[z, :, part] = values[0]
             rate_s[z, :, part] = jnp.where(inside, TIME_STEP / jnp.where(inside, values[1], 1.0), 0.0)
             mod[z + 1, :, part] = values[2] * inverse_shift[:, 0:cols]
             strain[z + 1, :, part] = values[3]
-            mask[z + 1, :, part] = jnp.where(inside, 1.0, 0.0)
+            mask[z + 1, :, part] = jnp.where(near >= 0, 1.0, 0.0)
             power = jnp.zeros(ids.shape, jnp.float32)
             for t in range(tiles):
                 power = jnp.where(patches == t, power_table[t], power)
@@ -285,15 +295,18 @@
         return flow_z
 
     blank = mod[0]
-    lax.fori_loop(0, layers, first_step, blank)
+    lax.fori_loop(0, layers, first_step, cond[layers])
 
     def second_step(z, flow_below):
         value, flow_z = heat(z, flow_below, temp2, False)
         warmed[z] = value[HALO : HALO + rows, 0:cols]
-        strain[z + 1] = strain[z + 1] * value
+        strain[z + 1] = strain[z + 1] * value[kept]
         return flow_z
 
-    lax.fori_loop(0, layers, second_step, blank)
+    lax.fori_loop(0, layers, second_step, cond[layers])
+    results = [pltpu.make_async_copy(warmed, warmed_out, out_sem.at[0])]
+    results[0].start()
+
 
     def matrix_planes(p):
         f = mod[p]
@@ -316,8 +329,7 @@
 
     stream(layers, 6, blank, matrix_planes, matrix_emit, 0)
 
-    def fold(value):
-        inner = value[HALO : HALO + rows, 0:cols]
+    def fold(inner):
         result = inner[0:8]
         for r in range(8, rows, 8):
             result = result + inner[r : r + 8]
@@ -335,10 +347,12 @@
         for c in range(3):
             value = -inside * (m * out[c] + s * out[3 + c] + out[6 + c])
             v[0, c, p] = value
-            acc = acc + fold(value * value)
+            inner = value[inner_rows, 0:cols]
+            vown[0, c, p] = inner
+            acc = acc + fold(inner * inner)
         return acc
 
-    moments = [stream(layers, 9, blank, load_planes, load_emit, tile)]
+    moment_s[0] = stream(layers, 9, blank, load_planes, load_emit, tile)
 
     def shares(k):
         found = []
@@ -346,7 +360,7 @@
             there = lax.rem(iz + step, nz)
             found.append(
                 pltpu.make_async_remote_copy(
-                    src_ref=v.at[k, :, pl.ds(1 + there * share, share), pl.ds(HALO, rows), pl.ds(0, cols)],
+                    src_ref=vown.at[k, :, pl.ds(1 + there * share, share)],
                     dst_ref=vrecv.at[k, step - 1],
                     send_sem=vsend_sem.at[k, step - 1], recv_sem=vrecv_sem.at[k, step - 1],
                     device_id=(ix, iy, there), device_id_type=MESH,
@@ -354,22 +368,24 @@
             )
         return found
 
-    sharing = [shares(k) for k in range(ITERS + 1)]
-    for copy in sharing[0]:
-        copy.start()
-
-    for k in range(ITERS):
-        def planes(p, k=k):
+    def share_basis(k):
+        for copy in shares(k):
+            copy.start()
+
+    share_basis(0)
+
+    def apply(k, width):
+        def planes(p):
             m = mod[p]
             u = [v[k, c, p] for c in range(3)]
-            first = vector_stencil(*u)
-            second = vector_stencil(*[m * f for f in u])
+            first = vector_stencil(*u, width)
+            second = vector_stencil(*[m * f for f in u], width)
             return tuple(a + b for a, b in zip(first, second))
 
-        def emit(p, out, acc, k=k):
-            m, inside = mod[p], mask[p]
-            u = [v[k, c, p] for c in range(3)]
-            zz, xx, yy, zx, zy, xy = [mats[c, p] for c in range(6)]
+        def emit(p, out, acc):
+            m = mod[p, :, 0:width]
+            u = [v[k, c, p, :, 0:width] for c in range(3)]
+            zz, xx, yy, zx, zy, xy = [mats[c, p, :, 0:width] for c in range(6)]
             grown = (
                 zz * u[0] + zx * u[1] + zy * u[2],
                 zx * u[0] + xx * u[1] + xy * u[2],
@@ -377,22 +393,32 @@
             )
             odd, even = acc
             for c in range(3):
-                value = inside * (grown[c] - m * out[c] - out[3 + c])
-                v[k + 1, c, p] = value
-                odd = odd + fold(value * u[c])
-                even = even + fold(value * value)
+                value = grown[c] - m * out[c] - out[3 + c]
+                if width > cols:
+                    value = mask[p] * value
+                    v[k + 1, c, p] = value
+                inner = value[inner_rows, 0:cols]
+                vown[k + 1, c, p] = inner
+                odd = odd + fold(inner * vown[k, c, p])
+                even = even + fold(inner * inner)
             return odd, even
 
-        odd, even = stream(layers, 6, blank, planes, emit, (tile, tile))
-        moments += [odd, even]
-        for copy in sharing[k + 1]:
-            copy.start()
-
-    moments = moments[: 2 * ITERS]
+        odd, even = stream(layers, 6, mod[0, :, 0:width], planes, emit, (tile, tile))
+        moment_s[2 * k + 1] = odd
+        moment_s[2 * k + 2] = even
+
+    def grow(k, _):
+        apply(k, 2 * cols)
+        share_basis(k + 1)
+        return 0
+
+    lax.fori_loop(0, ITERS - 1, grow, 0)
+    apply(ITERS - 1, cols)
+
     lane8 = lax.broadcasted_iota(jnp.int32, (1, cols), 1)
     row = jnp.zeros((1, cols), jnp.float32)
-    for k, value in enumerate(moments):
-        line = jnp.sum(value, axis=0, keepdims=True)
+    for k in range(2 * ITERS):
+        line = jnp.sum(moment_s[k], axis=0, keepdims=True)
         row = jnp.where(lane8 == k, jnp.sum(line, axis=1, keepdims=True), row)
     red_src[...] = row
     red_buf[me] = row
@@ -424,6 +450,7 @@
         return 0
 
     lax.fori_loop(1, total, start, 0)
+    share_basis(ITERS)
     lax.fori_loop(1, total, finish, 0)
 
     def add(k, acc):
@@ -469,20 +496,16 @@
             rr = new
     res = [shift_scalar * x for x in res]
 
-    for k in range(ITERS + 1):
-        for copy in sharing[k]:
-            copy.wait_recv()
-
     for step in range(nz):
         where = pl.ds(pl.multiple_of(lax.rem(iz + nz - step, nz) * cols, cols), cols)
+        if step:
+            for k in range(size):
+                shares(k)[step - 1].wait_recv()
 
         def combine(z, _, step=step, where=where):
             for c in range(3):
                 if step == 0:
-                    parts = [
-                        v[k, c, 1 + iz * share + z, pl.ds(HALO, rows), pl.ds(0, cols)]
-                        for k in range(size)
-                    ]
+                    parts = [vown[k, c, 1 + iz * share + z] for k in range(size)]
                 else:
                     parts = [vrecv[k, step - 1, c, z] for k in range(size)]
                 total_s = sol[0] * parts[0]
@@ -491,11 +514,18 @@
                     if sol[k] is not None:
                         total_s = total_s + sol[k] * parts[k]
                     total_r = total_r + res[k] * parts[k]
-                solution[c, z, :, where] = total_s
-                residual[c, z, :, where] = total_r
+                solution[step, c, z] = total_s
+                residual[step, c, z] = total_r
             return 0
 
         lax.fori_loop(0, share, combine, 0)
+        for index, (a, b) in enumerate(((solution, solution_out), (residual, residual_out))):
+            results.append(
+                pltpu.make_async_copy(
+                    a.at[step], b.at[:, :, :, where], out_sem.at[1 + 2 * step + index]
+                )
+            )
+            results[-1].start()
 
     for target, _, copies, _, _ in moves:
         @pl.when(target)
@@ -503,9 +533,11 @@
             for copy in copies:
                 copy.wait_send()
     for k in range(ITERS + 1):
-        for copy in sharing[k]:
+        for copy in shares(k):
             copy.wait_send()
     lax.fori_loop(1, total, sent, 0)
+    for copy in results:
+        copy.wait()
 
 
 def per_device(sizes, *arrays):
@@ -519,19 +551,24 @@
     dma = pltpu.SemaphoreType.DMA
     out = jax.ShapeDtypeStruct((3, share, rows, cols * nz), f32)
     plane = vmem((layers, *ext), f32)
-    padded = vmem((layers + 2, *ext), f32)
+    kept = (rows + 2 * EDGE, 2 * cols)
+    padded = vmem((layers + 2, *kept), f32)
+    half = vmem((nz, 3, share, rows, cols), f32)
     return pl.pallas_call(
         functools.partial(kernel, sizes),
         out_shape=(jax.ShapeDtypeStruct((layers, rows, cols), f32), out, out),
-        in_specs=[pl.BlockSpec(memory_space=pltpu.VMEM)] * 3
+        in_specs=[pl.BlockSpec(memory_space=pl.ANY)] * 3
         + [pl.BlockSpec(memory_space=pltpu.SMEM)] * 2,
-        out_specs=[pl.BlockSpec(memory_space=pltpu.VMEM)] * 3,
+        out_specs=[pl.BlockSpec(memory_space=pl.ANY)] * 3,
         scratch_shapes=[
+            vmem((layers, rows, cols), f32), half, half,
+            vmem((ITERS + 1, 3, layers + 1, rows, cols), f32),
+            vmem((2 * ITERS + 1, 8, cols), f32), dma((1 + 2 * nz,)),
             plane, plane, vmem((layers, *ext), i32), vmem((layers, *ext), i32),
             vmem((layers + 1, *ext), f32), padded, padded, padded,
             plane, plane, plane, plane, plane,
-            vmem((6, layers + 1, *ext), f32),
-            vmem((ITERS + 1, 3, layers + 2, *ext), f32),
+            vmem((6, layers + 1, *kept), f32),
+            vmem((ITERS, 3, layers + 2, *kept), f32),
             vmem((ITERS + 1, nz - 1, 3, share, rows, cols), f32),
             vmem((2, rows, cols), f32), vmem((2, 2, rows, cols), i32),
             vmem((2, ext[0], cols), f32), vmem((2, 2, ext[0], cols), i32),
@@ -540,7 +577,7 @@
             dma((ITERS + 1, nz - 1)), dma((ITERS + 1, nz - 1)), dma((total,)), dma((total,)),
         ],
         compiler_params=pltpu.CompilerParams(
-            collective_id=0, has_side_effects=True, vmem_limit_bytes=60 * 1024 * 1024
+            collective_id=0, has_side_effects=True, vmem_limit_bytes=40 * 1024 * 1024
         ),
     )(*arrays)
 

time: 65.7 us -> 58.2 us (0.89)
  Pallas kernels: 60.7 us -> 51.1 us
  local copies, waits for them, and re-layouts: 4.13 us -> 6.19 us
    pallas_call x1, Pallas kernels: 60.7 us -> 51.1 us  [per_device(): pl.pallas_call(functools.partial(kernel, sizes), out_shape=(jax.ShapeDtyp...]
    unnamed x5 -> x13, local copies, waits for them, and re-layouts: 4.13 us -> 6.19 us
where the time goes in v2:
time: 58.2 us; the launch traced here: 58 us
  Pallas kernels  51.1 us (88%)
  local copies, waits for them, and re-layouts  6.19 us (11%)
  between operations  0.65 us (1%)
    pallas_call x1, Pallas kernels, per_device(): pl.pallas_call(functools.partial(kernel, sizes), out_shape=(jax.ShapeDtyp...  51.1 us
    unnamed x13, local copies, waits for them, and re-layouts  6.19 us

profile of v2, /device:TPU:0, one launch (start us, length us, event | category | flops | bytes accessed | tf_op | source)
XLA Modules:
  0.0 58.0 jit_solution(15196884421535639874)
XLA Ops:
  0.6 0.0 copy-start
  0.6 0.9 %copy-done = f32[16,16,128]{2,1,0:T(8,128)S(1)} copy-done((f32[16,16,128]{2,1,0:T(8,128)S(1)}, f32[16,16,128]{2,1,0:T(8,128)}, u32[]{:S(2)}) %copy-start) | copy-done | bytes 131096
  1.5 0.0 copy-start.1
  1.5 0.9 %copy-done.1 = s32[16,16,128]{2,1,0:T(8,128)S(1)} copy-done((s32[16,16,128]{2,1,0:T(8,128)S(1)}, s32[16,16,128]{2,1,0:T(8,128)}, u32[]{:S(2)}) %copy-start.1) | copy-done | bytes 131096
  2.4 0.0 copy-start.2
  2.4 0.9 %copy-done.2 = s32[16,16,128]{2,1,0:T(8,128)S(1)} copy-done((s32[16,16,128]{2,1,0:T(8,128)S(1)}, s32[16,16,128]{2,1,0:T(8,128)}, u32[]{:S(2)}) %copy-start.2) | copy-done | bytes 131096
  3.3 0.0 copy-start.3
  3.3 0.7 %copy-done.3 = f32[4,4]{1,0:T(4,128)S(1)} copy-done((f32[4,4]{1,0:T(4,128)S(1)}, f32[4,4]{1,0:T(4,128)}, u32[]{:S(2)}) %copy-start.3) | copy-done | bytes 88
  4.0 0.0 copy-start.4
  4.0 0.7 %copy-done.4 = f32[16]{0:T(128)S(1)} copy-done((f32[16]{0:T(128)S(1)}, f32[16]{0:T(128)}, u32[]{:S(2)}) %copy-start.4) | copy-done | bytes 88
  4.7 51.1 %shard_map.76 = (f32[16,16,128]{2,1,0:T(8,128)S(1)}, f32[3,8,16,256]{3,2,1,0:T(8,128)S(1)}, f32[3,8,16,256]{3,2,1,0:T(8,128)S(1)}) custom-call(f32[16,16,128]{2,1,0:T(8,128)S(1)} %copy-done, s32[16,16,128]{2,1,0:T(8,128)S(1)} %copy-done.1, s32[16,16,128]{2,1,0:T(8,128)S(1)} %copy-done.2, f32[4,4]{1,0:T(4,128)S(1)} %copy-done.3, f32[16]{0:T(128)S(1)} %copy-done.4), custom_call_target="tpu_custom_call" | custom-call | tf_op jit(solution)/shard_map/pallas_call | solution.py:557
  55.8 0.7 %copy.11 = f32[16,16,128]{2,1,0:T(8,128)} copy(f32[16,16,128]{2,1,0:T(8,128)S(1)} %get-tuple-element.6) | data formatting | bytes 262144
  56.5 0.7 %copy.12 = f32[3,8,16,256]{3,2,1,0:T(8,128)} copy(f32[3,8,16,256]{3,2,1,0:T(8,128)S(1)} %get-tuple-element.7) | data formatting | bytes 786432
  57.2 0.7 %copy.13 = f32[3,8,16,256]{3,2,1,0:T(8,128)} copy(f32[3,8,16,256]{3,2,1,0:T(8,128)S(1)} %get-tuple-element.8) | data formatting | bytes 786432
Async XLA Ops:
  0.6 0.9 %copy-start = (f32[16,16,128]{2,1,0:T(8,128)S(1)}, f32[16,16,128]{2,1,0:T(8,128)}, u32[]{:S(2)}) copy-start(f32[16,16,128]{2,1,0:T(8,128)} %kelvin.1) | copy-start | bytes 393220
  1.5 0.9 %copy-start.1 = (s32[16,16,128]{2,1,0:T(8,128)S(1)}, s32[16,16,128]{2,1,0:T(8,128)}, u32[]{:S(2)}) copy-start(s32[16,16,128]{2,1,0:T(8,128)} %label.1) | copy-start | bytes 393220
  2.4 0.9 %copy-start.2 = (s32[16,16,128]{2,1,0:T(8,128)S(1)}, s32[16,16,128]{2,1,0:T(8,128)}, u32[]{:S(2)}) copy-start(s32[16,16,128]{2,1,0:T(8,128)} %patch.1) | copy-start | bytes 393220
  3.3 0.7 %copy-start.3 = (f32[4,4]{1,0:T(4,128)S(1)}, f32[4,4]{1,0:T(4,128)}, u32[]{:S(2)}) copy-start(f32[4,4]{1,0:T(4,128)} %traits.1) | copy-start | bytes 196
  4.0 0.7 %copy-start.4 = (f32[16]{0:T(128)S(1)}, f32[16]{0:T(128)}, u32[]{:S(2)}) copy-start(f32[16]{0:T(128)} %power_table.1) | copy-start | bytes 196

commit v3 on v2

--- a/solution.py
+++ b/solution.py
@@ -96,9 +96,9 @@
 
 def kernel(
     sizes,
-    kelvin, label, patch, traits, power_table,
+    kelvin, label, patch, traits_in, power_in,
     warmed_out, solution_out, residual_out,
-    warmed, solution, residual, vown, moment_s, out_sem,
+    traits, power_table, table_sem, warmed, solution, residual, vown, moment_s, out_sem,
     temp, temp2, lab, pat, cond, mod, strain, mask, gx_s, gy_s, gz_s, rate_s, pow_s, mats,
     v, vrecv, pack_f, pack_i, got_f, got_i, red_src, red_buf,
     local_sem, send_sem, recv_sem, vsend_sem, vrecv_sem, rsend_sem, rrecv_sem,
@@ -133,26 +133,14 @@
         pltpu.make_async_copy(a, b.at[own], local_sem.at[i])
         for i, (a, b) in enumerate(((kelvin, temp), (label, lab), (patch, pat)))
     ]
-    for copy in local:
+    tables = [
+        pltpu.make_async_copy(traits_in, traits, table_sem.at[0]),
+        pltpu.make_async_copy(power_in, power_table, table_sem.at[1]),
+    ]
+    for copy in local + tables:
         copy.start()
 
-    lane = lax.broadcasted_iota(jnp.int32, (rows, cols), 1)
     sources = (kelvin, label, patch)
-    for copy in local:
-        copy.wait()
-    for side in (0, 1):
-        for index, ref in enumerate((temp, lab, pat)):
-            packed = jnp.zeros((rows, cols), ref.dtype)
-            for z in range(layers):
-                amount = (HALO * z + (HALO if side else 0)) % cols
-                piece = ref[(z, *own[1:])]
-                piece = pltpu.roll(piece, amount, 1) if amount else piece
-                packed = jnp.where(lane // HALO == z, piece, packed)
-            if index == 0:
-                pack_f[side] = packed
-            else:
-                pack_i[side, index - 1] = packed
-
     pl.semaphore_wait(barrier, total - 1)
 
     def transfers(number):
@@ -191,7 +179,35 @@
         return target, origin, copies, to_rows, dc
 
     moves = [transfers(i) for i in range(len(DIRECTIONS))]
-    for target, _, copies, _, _ in moves:
+    for target, _, copies, _, dc in moves:
+        if dc != 0:
+            continue
+
+        @pl.when(target)
+        def _(copies=copies):
+            for copy in copies:
+                copy.start()
+
+    lane = lax.broadcasted_iota(jnp.int32, (rows, cols), 1)
+    for copy in local:
+        copy.wait()
+    for side in (0, 1):
+        for index, ref in enumerate((temp, lab, pat)):
+            packed = jnp.zeros((rows, cols), ref.dtype)
+            for z in range(layers):
+                amount = (HALO * z + (HALO if side else 0)) % cols
+                piece = ref[(z, *own[1:])]
+                piece = pltpu.roll(piece, amount, 1) if amount else piece
+                packed = jnp.where(lane // HALO == z, piece, packed)
+            if index == 0:
+                pack_f[side] = packed
+            else:
+                pack_i[side, index - 1] = packed
+
+    for target, _, copies, _, dc in moves:
+        if dc == 0:
+            continue
+
         @pl.when(target)
         def _(copies=copies):
             for copy in copies:
@@ -224,6 +240,8 @@
         mats[c, 0] = blank_kept
     cond[layers] = empty
 
+    for copy in tables:
+        copy.wait()
     shift_scalar = 3.0 * (traits[2, 0] + traits[2, 1] + traits[2, 2] + traits[2, 3])
     inverse_shift = 1.0 / jnp.full((1, 2 * cols), shift_scalar, jnp.float32)
 
@@ -269,7 +287,7 @@
             pow_s[z, :, part] = power
         return 0
 
-    lax.fori_loop(0, layers, prepare, 0)
+    lax.fori_loop(0, layers, prepare, 0, unroll=2)
 
     def conduct(a, b):
         return 2.0 * a * b / jnp.maximum(a + b, 0.25)
@@ -295,7 +313,7 @@
         return flow_z
 
     blank = mod[0]
-    lax.fori_loop(0, layers, first_step, cond[layers])
+    lax.fori_loop(0, layers, first_step, cond[layers], unroll=4)
 
     def second_step(z, flow_below):
         value, flow_z = heat(z, flow_below, temp2, False)
@@ -303,7 +321,7 @@
         strain[z + 1] = strain[z + 1] * value[kept]
         return flow_z
 
-    lax.fori_loop(0, layers, second_step, cond[layers])
+    lax.fori_loop(0, layers, second_step, cond[layers], unroll=4)
     results = [pltpu.make_async_copy(warmed, warmed_out, out_sem.at[0])]
     results[0].start()
 
@@ -518,7 +536,7 @@
                 residual[step, c, z] = total_r
             return 0
 
-        lax.fori_loop(0, share, combine, 0)
+        lax.fori_loop(0, share, combine, 0, unroll=2)
         for index, (a, b) in enumerate(((solution, solution_out), (residual, residual_out))):
             results.append(
                 pltpu.make_async_copy(
@@ -557,10 +575,10 @@
     return pl.pallas_call(
         functools.partial(kernel, sizes),
         out_shape=(jax.ShapeDtypeStruct((layers, rows, cols), f32), out, out),
-        in_specs=[pl.BlockSpec(memory_space=pl.ANY)] * 3
-        + [pl.BlockSpec(memory_space=pltpu.SMEM)] * 2,
+        in_specs=[pl.BlockSpec(memory_space=pltpu.HBM)] * 5,
         out_specs=[pl.BlockSpec(memory_space=pl.ANY)] * 3,
         scratch_shapes=[
+            pltpu.SMEM(arrays[3].shape, f32), pltpu.SMEM(arrays[4].shape, f32), dma((2,)),
             vmem((layers, rows, cols), f32), half, half,
             vmem((ITERS + 1, 3, layers + 1, rows, cols), f32),
             vmem((2 * ITERS + 1, 8, cols), f32), dma((1 + 2 * nz,)),
@@ -579,7 +597,7 @@
         compiler_params=pltpu.CompilerParams(
             collective_id=0, has_side_effects=True, vmem_limit_bytes=40 * 1024 * 1024
         ),
-    )(*arrays)
+    )(*[pltpu.with_memory_space_constraint(a, pltpu.HBM) for a in arrays])
 
 
 def solution(mesh):

time: 58.2 us -> 49.8 us (0.86)
  Pallas kernels: 51.1 us -> 46.9 us
  local copies, waits for them, and re-layouts: 6.19 us -> 2.15 us
    pallas_call x1, Pallas kernels: 51.1 us -> 46.9 us  [per_device(): pl.pallas_call(functools.partial(kernel, sizes), out_shape=(jax.ShapeDtyp...]
    unnamed x13 -> x3, local copies, waits for them, and re-layouts: 6.19 us -> 2.15 us
where the time goes in v3:
time: 49.8 us; the launch traced here: 49.7 us
  Pallas kernels  46.9 us (94%)
  local copies, waits for them, and re-layouts  2.15 us (4%)
  between operations  0.64 us (1%)
    pallas_call x1, Pallas kernels, per_device(): pl.pallas_call(functools.partial(kernel, sizes), out_shape=(jax.ShapeDtyp...  46.9 us
    unnamed x3, local copies, waits for them, and re-layouts  2.15 us

profile of v3, /device:TPU:0, one launch (start us, length us, event | category | flops | bytes accessed | tf_op | source)
XLA Modules:
  0.0 49.7 jit_solution(4964953932348512831)
XLA Ops:
  0.6 46.9 %shard_map.76 = (f32[16,16,128]{2,1,0:T(8,128)S(1)}, f32[3,8,16,256]{3,2,1,0:T(8,128)S(1)}, f32[3,8,16,256]{3,2,1,0:T(8,128)S(1)}) custom-call(f32[16,16,128]{2,1,0:T(8,128)} %kelvin.1, s32[16,16,128]{2,1,0:T(8,128)} %label.1, s32[16,16,128]{2,1,0:T(8,128)} %patch.1, f32[4,4]{1,0:T(4,128)} %traits_in.1, f32[16]{0:T(128)} %power_in.1), custom_call_target="tpu_custom_call" | custom-call | tf_op jit(solution)/shard_map/pallas_call | solution.py:575
  47.5 0.7 %copy.11 = f32[16,16,128]{2,1,0:T(8,128)} copy(f32[16,16,128]{2,1,0:T(8,128)S(1)} %get-tuple-element.6) | data formatting | bytes 262144
  48.2 0.7 %copy.12 = f32[3,8,16,256]{3,2,1,0:T(8,128)} copy(f32[3,8,16,256]{3,2,1,0:T(8,128)S(1)} %get-tuple-element.7) | data formatting | bytes 786432
  48.9 0.7 %copy.13 = f32[3,8,16,256]{3,2,1,0:T(8,128)} copy(f32[3,8,16,256]{3,2,1,0:T(8,128)S(1)} %get-tuple-element.8) | data formatting | bytes 786432

commit v4 on v3

--- a/solution.py
+++ b/solution.py
@@ -9,6 +9,7 @@
 
 ITERS = 3
 HALO = 8
+REACH = 6
 EDGE = 4
 TIME_STEP = 0.03
 ANCHOR = 0.5
@@ -91,7 +92,7 @@
         return held, below, extra
 
     zeros = [zero] * count
-    return lax.fori_loop(1, layers + 2, body, (zeros, list(zeros), extra))[2]
+    return lax.fori_loop(1, layers + 2, body, (zeros, list(zeros), extra), unroll=4)[2]
 
 
 def kernel(
@@ -155,9 +156,9 @@
         if dx == 0:
             from_rows, to_rows = pl.ds(0, rows), pl.ds(HALO, rows)
         elif dx == 1:
-            from_rows, to_rows = pl.ds(rows - HALO, HALO), pl.ds(0, HALO)
+            from_rows, to_rows = pl.ds(rows - REACH, REACH), pl.ds(HALO - REACH, REACH)
         else:
-            from_rows, to_rows = pl.ds(0, HALO), pl.ds(HALO + rows, HALO)
+            from_rows, to_rows = pl.ds(0, REACH), pl.ds(HALO + rows, REACH)
         if dc == 0:
             pairs = [
                 (ref.at[:, from_rows, :], ext.at[:, to_rows, pl.ds(0, cols)])

time: 49.8 us -> 44.8 us (0.90)
  Pallas kernels: 46.9 us -> 41.8 us
    pallas_call x1, Pallas kernels: 46.9 us -> 41.8 us  [per_device(): pl.pallas_call(functools.partial(kernel, sizes), out_shape=(jax.ShapeDtyp...]
where the time goes in v4:
time: 44.8 us; the launch traced here: 44.6 us
  Pallas kernels  41.8 us (93%)
  local copies, waits for them, and re-layouts  2.15 us (5%)
  between operations  0.64 us (1%)
    pallas_call x1, Pallas kernels, per_device(): pl.pallas_call(functools.partial(kernel, sizes), out_shape=(jax.ShapeDtyp...  41.8 us
    unnamed x3, local copies, waits for them, and re-layouts  2.15 us

profile of v4, /device:TPU:0, one launch (start us, length us, event | category | flops | bytes accessed | tf_op | source)
XLA Modules:
  0.0 44.6 jit_solution(6713162397818692774)
XLA Ops:
  0.6 41.8 %shard_map.76 = (f32[16,16,128]{2,1,0:T(8,128)S(1)}, f32[3,8,16,256]{3,2,1,0:T(8,128)S(1)}, f32[3,8,16,256]{3,2,1,0:T(8,128)S(1)}) custom-call(f32[16,16,128]{2,1,0:T(8,128)} %kelvin.1, s32[16,16,128]{2,1,0:T(8,128)} %label.1, s32[16,16,128]{2,1,0:T(8,128)} %patch.1, f32[4,4]{1,0:T(4,128)} %traits_in.1, f32[16]{0:T(128)} %power_in.1), custom_call_target="tpu_custom_call" | custom-call | tf_op jit(solution)/shard_map/pallas_call | solution.py:576
  42.5 0.7 %copy.11 = f32[16,16,128]{2,1,0:T(8,128)} copy(f32[16,16,128]{2,1,0:T(8,128)S(1)} %get-tuple-element.6) | data formatting | bytes 262144
  43.1 0.7 %copy.12 = f32[3,8,16,256]{3,2,1,0:T(8,128)} copy(f32[3,8,16,256]{3,2,1,0:T(8,128)S(1)} %get-tuple-element.7) | data formatting | bytes 786432
  43.9 0.7 %copy.13 = f32[3,8,16,256]{3,2,1,0:T(8,128)} copy(f32[3,8,16,256]{3,2,1,0:T(8,128)S(1)} %get-tuple-element.8) | data formatting | bytes 786432

commit v5 on v4

--- a/solution.py
+++ b/solution.py
@@ -127,7 +127,7 @@
         )
         return 0
 
-    lax.fori_loop(1, total, greet, 0)
+    lax.fori_loop(1, total, greet, 0, unroll=4)
 
     own = (slice(None), pl.ds(HALO, rows), pl.ds(0, cols))
     local = [
@@ -288,7 +288,7 @@
             pow_s[z, :, part] = power
         return 0
 
-    lax.fori_loop(0, layers, prepare, 0, unroll=2)
+    lax.fori_loop(0, layers, prepare, 0, unroll=4)
 
     def conduct(a, b):
         return 2.0 * a * b / jnp.maximum(a + b, 0.25)
@@ -468,14 +468,14 @@
         spread(k).wait_send()
         return 0
 
-    lax.fori_loop(1, total, start, 0)
+    lax.fori_loop(1, total, start, 0, unroll=4)
     share_basis(ITERS)
-    lax.fori_loop(1, total, finish, 0)
+    lax.fori_loop(1, total, finish, 0, unroll=4)
 
     def add(k, acc):
         return acc + red_buf[k]
 
-    summed = lax.fori_loop(0, total, add, jnp.zeros((1, cols), jnp.float32))
+    summed = lax.fori_loop(0, total, add, jnp.zeros((1, cols), jnp.float32), unroll=4)
     m = [
         jnp.sum(jnp.where(lane8 == k, summed, 0.0), axis=1, keepdims=True) for k in range(2 * ITERS)
     ]
@@ -517,31 +517,26 @@
 
     for step in range(nz):
         where = pl.ds(pl.multiple_of(lax.rem(iz + nz - step, nz) * cols, cols), cols)
-        if step:
-            for k in range(size):
-                shares(k)[step - 1].wait_recv()
-
-        def combine(z, _, step=step, where=where):
-            for c in range(3):
-                if step == 0:
-                    parts = [vown[k, c, 1 + iz * share + z] for k in range(size)]
-                else:
-                    parts = [vrecv[k, step - 1, c, z] for k in range(size)]
-                total_s = sol[0] * parts[0]
-                total_r = res[0] * parts[0]
-                for k in range(1, size):
-                    if sol[k] is not None:
-                        total_s = total_s + sol[k] * parts[k]
-                    total_r = total_r + res[k] * parts[k]
-                solution[step, c, z] = total_s
-                residual[step, c, z] = total_r
-            return 0
-
-        lax.fori_loop(0, share, combine, 0, unroll=2)
-        for index, (a, b) in enumerate(((solution, solution_out), (residual, residual_out))):
+        for index, (weights, held, target) in enumerate(
+            ((sol[:ITERS], solution, solution_out), (res, residual, residual_out))
+        ):
+            if step:
+                for k in range(ITERS) if index == 0 else (ITERS,):
+                    shares(k)[step - 1].wait_recv()
+
+            def combine(z, _, step=step, weights=weights, held=held):
+                for c in range(3):
+                    value = None
+                    for k, weight in enumerate(weights):
+                        part = vown[k, c, 1 + iz * share + z] if step == 0 else vrecv[k, step - 1, c, z]
+                        value = weight * part if value is None else value + weight * part
+                    held[step, c, z] = value
+                return 0
+
+            lax.fori_loop(0, share, combine, 0, unroll=4)
             results.append(
                 pltpu.make_async_copy(
-                    a.at[step], b.at[:, :, :, where], out_sem.at[1 + 2 * step + index]
+                    held.at[step], target.at[:, :, :, where], out_sem.at[1 + 2 * step + index]
                 )
             )
             results[-1].start()

time: 44.8 us -> 44.5 us (level)
  no operation moved by 1% of the time
where the time goes in v5:
time: 44.5 us; the launch traced here: 44.3 us
  Pallas kernels  41.6 us (93%)
  local copies, waits for them, and re-layouts  2.15 us (5%)
  between operations  0.64 us (1%)
    pallas_call x1, Pallas kernels, per_device(): pl.pallas_call(functools.partial(kernel, sizes), out_shape=(jax.ShapeDtyp...  41.6 us
    unnamed x3, local copies, waits for them, and re-layouts  2.15 us

profile of v5, /device:TPU:0, one launch (start us, length us, event | category | flops | bytes accessed | tf_op | source)
XLA Modules:
  0.0 44.3 jit_solution(15771596513227893704)
XLA Ops:
  0.6 41.6 %shard_map.76 = (f32[16,16,128]{2,1,0:T(8,128)S(1)}, f32[3,8,16,256]{3,2,1,0:T(8,128)S(1)}, f32[3,8,16,256]{3,2,1,0:T(8,128)S(1)}) custom-call(f32[16,16,128]{2,1,0:T(8,128)} %kelvin.1, s32[16,16,128]{2,1,0:T(8,128)} %label.1, s32[16,16,128]{2,1,0:T(8,128)} %patch.1, f32[4,4]{1,0:T(4,128)} %traits_in.1, f32[16]{0:T(128)} %power_in.1), custom_call_target="tpu_custom_call" | custom-call | tf_op jit(solution)/shard_map/pallas_call | solution.py:571
  42.2 0.7 %copy.11 = f32[16,16,128]{2,1,0:T(8,128)} copy(f32[16,16,128]{2,1,0:T(8,128)S(1)} %get-tuple-element.6) | data formatting | bytes 262144
  42.9 0.7 %copy.12 = f32[3,8,16,256]{3,2,1,0:T(8,128)} copy(f32[3,8,16,256]{3,2,1,0:T(8,128)S(1)} %get-tuple-element.7) | data formatting | bytes 786432
  43.6 0.7 %copy.13 = f32[3,8,16,256]{3,2,1,0:T(8,128)} copy(f32[3,8,16,256]{3,2,1,0:T(8,128)S(1)} %get-tuple-element.8) | data formatting | bytes 786432
